TPU v7x, 32 devices: a whole 2x2x4 slice. The times are simulated.
32 devices in a mesh: ctx: 8 (over z, core), head: 4 (over y, x).
Axes of the slice: x: 2, y: 2, z: 4, core: 2. Of those that a mesh axis runs over, the one named last changes fastest.
Arguments:
- q_latent: bfloat16 [1024, 128, 512], P('ctx', 'head'), may hold values from -4 to 4
- q_rope: bfloat16 [1024, 8192], P('ctx', 'head'), may hold values from -5 to 5
- latent: bfloat16 [1024, 512], P('ctx'), may hold values from -5 to 5
- key_rope: bfloat16 [1024, 64], P('ctx'), may hold values from -5 to 5
- out_grad: bfloat16 [1024, 128, 512], P('ctx', 'head'), may hold values from -5 to 5
- inputs: bfloat16 [1024, 7168], P('ctx', 'head'), may hold values from -5 to 5
- doc_ids: int32 [1024], replicated, may hold values from 0 to 7, never falling along the last dimension, each value on 1 to 256 neighbouring positions
Outputs:
- q_latent_grad: bfloat16 [1024, 128, 512], P('ctx', 'head')
- q_rope_grad: bfloat16 [1024, 8192], P('ctx', 'head')
- latent_grad: bfloat16 [1024, 512], P('ctx')
- key_rope_grad: bfloat16 [1024, 64], P('ctx')
- proj_grad: float32 [512, 7168], P('ctx', 'head')
Inputs may be any that keep to these rules, and one draw needn't show every extreme that they name: `doc_ids`: ids never fall along the sequence; each document has at most 256 positions.
All inputs are finite; a program needn't handle non-finite values.
Results may differ from a plain program's by a relative error of at most 0.0058.
Values may be sent and summed in bfloat16 or wider, within the bound.
No kernel may reach another device: no remote copies, remote signals or barrier semaphores. Data moves between devices by JAX's collectives and lax.ppermute only.
A program may use at most 128 MiB of HBM per device.

v0:
```python
import jax
import jax.numpy as jnp
from jax import lax
from jax.sharding import PartitionSpec as P

WIN_BLK = 3


softmax_scale = 192.0 ** (-0.5)


def passed_along(array, axis, by):
    peers = lax.axis_size(axis)
    pairs = [(i, i + by) for i in range(peers) if 0 <= i + by < peers]
    return lax.ppermute(array, axis, pairs)


def shards(q_latent, q_rope, latent, key_rope, out_grad, inputs, doc_ids):
    tok = latent.shape[0]
    heads_here = q_latent.shape[1]
    rope_width = key_rope.shape[1]
    lat_width = latent.shape[1]
    depth = WIN_BLK
    window = depth * tok
    rank = lax.axis_index("ctx")
    earlier = []
    for back in range(depth, 0, -1):
        earlier.append(passed_along((latent, key_rope), "ctx", back))
    keys_lat = jnp.concatenate([pair[0] for pair in earlier] + [latent], axis=0)
    keys_rope = jnp.concatenate([pair[1] for pair in earlier] + [key_rope], axis=0)
    start = rank * tok
    doc_pad = jnp.concatenate([jnp.full((window,), -1, jnp.int32), doc_ids], axis=0)
    key_doc = lax.dynamic_slice_in_dim(doc_pad, start, window + tok, 0)
    query_doc = lax.dynamic_slice_in_dim(doc_ids, start, tok, 0)
    qpos = jnp.arange(tok, dtype=jnp.int32)
    kpos = jnp.arange(window + tok, dtype=jnp.int32) - window
    allowed = (
        (kpos[None, :] <= qpos[:, None])
        & (qpos[:, None] - kpos[None, :] < window)
        & (key_doc[None, :] == query_doc[:, None])
    )
    qrope_heads = q_rope.reshape(tok, heads_here, rope_width)
    scores = (
        jnp.einsum("thj,kj->thk", q_latent, keys_lat, preferred_element_type=jnp.float32)
        + jnp.einsum("thr,kr->thk", qrope_heads, keys_rope, preferred_element_type=jnp.float32)
    ) * softmax_scale
    masked = jnp.where(allowed[:, None, :], scores, -jnp.inf)
    top = jnp.max(masked, axis=-1, keepdims=True)
    expo = jnp.exp(masked - top)
    probs = expo / jnp.sum(expo, axis=-1, keepdims=True)
    probs_low = probs.astype(jnp.bfloat16)
    merged = jnp.einsum("thk,kj->thj", probs_low, keys_lat, preferred_element_type=jnp.float32)
    delta = jnp.sum(out_grad * merged, axis=-1)
    dprob = jnp.einsum("thj,kj->thk", out_grad, keys_lat, preferred_element_type=jnp.float32)
    dscore = (probs * (dprob - delta[..., None]) * softmax_scale).astype(jnp.bfloat16)
    q_latent_grad = jnp.einsum(
        "thk,kj->thj", dscore, keys_lat, preferred_element_type=jnp.float32
    ).astype(jnp.bfloat16)
    q_rope_grad = jnp.einsum("thk,kr->thr", dscore, keys_rope, preferred_element_type=jnp.float32)
    q_rope_grad = q_rope_grad.reshape(tok, heads_here * rope_width).astype(jnp.bfloat16)
    part_lat = jnp.einsum(
        "thk,thj->kj", dscore, q_latent, preferred_element_type=jnp.float32
    ) + jnp.einsum("thk,thj->kj", probs_low, out_grad, preferred_element_type=jnp.float32)
    part_rope = jnp.einsum("thk,thr->kr", dscore, qrope_heads, preferred_element_type=jnp.float32)
    blocks_lat = part_lat.reshape(depth + 1, tok, lat_width)
    blocks_rope = part_rope.reshape(depth + 1, tok, rope_width)
    share_lat, share_rope = (
        lax.psum_scatter(blocks_lat, "head", scatter_dimension=1, tiled=True),
        lax.psum_scatter(blocks_rope, "head", scatter_dimension=1, tiled=True),
    )
    own_lat = share_lat[depth]
    own_rope = share_rope[depth]
    for back in range(1, depth + 1):
        got_lat, got_rope = passed_along(
            (share_lat[depth - back], share_rope[depth - back]), "ctx", -back
        )
        own_lat = own_lat + got_lat
        own_rope = own_rope + got_rope
    latent_grad, key_rope_grad = (
        lax.all_gather(own_lat.astype(jnp.bfloat16), "head", axis=0, tiled=True),
        lax.all_gather(own_rope.astype(jnp.bfloat16), "head", axis=0, tiled=True),
    )
    proj_grad = lax.psum_scatter(
        lax.dot_general(
            latent_grad, inputs, (((0,), (0,)), ((), ())), preferred_element_type=jnp.float32
        ),
        "ctx",
        scatter_dimension=0,
        tiled=True,
    )
    return (q_latent_grad, q_rope_grad, latent_grad, key_rope_grad, proj_grad)


def solution(mesh):
    placed = (
        P("ctx", "head", None),
        P("ctx", "head"),
        P("ctx", None),
        P("ctx", None),
        P("ctx", "head", None),
        P("ctx", "head"),
        P(),
    )
    return jax.shard_map(
        shards,
        mesh=mesh,
        in_specs=placed,
        out_specs=(
            P("ctx", "head", None),
            P("ctx", "head"),
            P("ctx", None),
            P("ctx", None),
            P("ctx", "head"),
        ),
        check_vma=False,
    )
```

profile of v0, /device:TPU:0, one launch (start us, length us, event | category | flops | bytes accessed | tf_op | source)
XLA Modules:
  0.0 199.9 jit_solution(8502988981172908835)
XLA Ops:
  7.2 4.5 %collective-permute-start.3 = (bf16[128,64]{0,1:T(8,128)(2,1)}, bf16[128,64]{0,1:T(8,128)(2,1)S(1)}, u32[]{:S(2)}, u32[]{:S(2)}) collective-permute-start(bf16[128,64]{0,1:T(8,128)(2,1)} %param.10), channel_id=1, source_target_pairs={{0,12},{4,16},{8,20},{12,24},{16,28},{1,13},{5,17},{9,21},{13,25},... | collective-permute-start | bytes 49160 | tf_op jit(solution)/shard_map/ppermute | solution.py:15
  11.8 3.5 %collective-permute-start.4 = (bf16[128,64]{0,1:T(8,128)(2,1)}, bf16[128,64]{0,1:T(8,128)(2,1)S(1)}, u32[]{:S(2)}, u32[]{:S(2)}) collective-permute-start(bf16[128,64]{0,1:T(8,128)(2,1)} %param.10), channel_id=1, source_target_pairs={{0,8},{4,12},{8,16},{12,20},{16,24},{20,28},{1,9},{5,13},{9,17},{1... | collective-permute-start | bytes 49160 | tf_op jit(solution)/shard_map/ppermute | solution.py:15
  15.3 3.3 %collective-permute-start.5 = (bf16[128,64]{0,1:T(8,128)(2,1)}, bf16[128,64]{0,1:T(8,128)(2,1)S(1)}, u32[]{:S(2)}, u32[]{:S(2)}) collective-permute-start(bf16[128,64]{0,1:T(8,128)(2,1)} %param.10), channel_id=1, source_target_pairs={{0,4},{4,8},{8,12},{12,16},{16,20},{20,24},{24,28},{1,5},{5,9},{9,... | collective-permute-start | bytes 49160 | tf_op jit(solution)/shard_map/ppermute | solution.py:15
  18.6 1.8 collective-permute-start
  20.4 1.7 collective-permute-start.1
  23.9 1.3 copy.27
  25.2 2.3 %collective-permute-start.2 = (bf16[128,512]{1,0:T(8,128)(2,1)}, bf16[128,512]{1,0:T(8,128)(2,1)S(1)}, u32[]{:S(2)}, u32[]{:S(2)}) collective-permute-start(bf16[128,512]{1,0:T(8,128)(2,1)} %param.9), channel_id=1, source_target_pairs={{0,4},{4,8},{8,12},{12,16},{16,20},{20,24},{24,28},{1,5},{5,9},{9,... | collective-permute-start | bytes 393224 | tf_op jit(solution)/shard_map/ppermute | solution.py:15
  27.5 2.0 fusion.41
  29.5 9.6 %fusion.7 = (f32[128,32]{0,1:T(8,128)S(1)}, f32[512,128,32]{1,0,2:T(8,128)S(1)}) fusion(pred[128,512]{0,1:T(8,128)(4,1)S(1)} %fusion.34, f32[512,128,32]{1,0,2:T(8,128)S(1)} %fusion.41, bf16[128,32,512]{2,1,0:T(8,128)(2,1)} %param.7, bf16[128,512]{1,0:T(8,128)(2,1)S(1)} %copy-done.3, bf16[128,512]{1,0:T(8,128)(2,1)S(1)} %collective-permute-done.2, ...), kind=kOutput, calls=%fused_computation.14 | convolution fusion | flops 2157965312 | bytes 21577728 | tf_op jit(solution)/shard_map/thj,kj->thk/dot_general | solution.py:44
  39.1 1.6 fusion.9
  40.8 3.6 %copy-done.5 = bf16[128,32,512]{2,1,0:T(8,128)(2,1)S(1)} copy-done((bf16[128,32,512]{2,1,0:T(8,128)(2,1)S(1)}, bf16[128,32,512]{2,1,0:T(8,128)(2,1)}, u32[]{:S(2)}) %copy-start.5) | copy-done | bytes 4194328
  44.4 7.6 %fusion.22 = f32[512,512]{1,0:T(8,128)S(1)} fusion(bf16[128,32,512]{2,1,0:T(8,128)(2,1)S(1)} %copy-done.5, f32[512,128,32]{1,0,2:T(8,128)S(1)} %get-tuple-element.22, f32[128,32]{0,1:T(8,128)S(1)} %fusion.9, f32[128,32]{0,1:T(8,128)S(1)} %get-tuple-element.21, pred[128,512]{0,1:T(8,128)(4,1)S(1)} %fusion.34), kind=kOutput, calls=%fused_computation.28 | convolution fusion | flops 2155872256 | bytes 13729792 | tf_op jit(solution)/shard_map/thk,thj->kj/dot_general | solution.py:63
  52.0 7.4 %multiply_reduce_fusion = f32[128,32]{0,1:T(8,128)S(1)} fusion(bf16[128,32,512]{2,1,0:T(8,128)(2,1)S(1)} %copy-done.5, bf16[128,512]{1,0:T(8,128)(2,1)S(1)} %copy-done.3, bf16[128,512]{1,0:T(8,128)(2,1)S(1)} %collective-permute-done.2, bf16[128,512]{1,0:T(8,128)(2,1)S(1)} %collective-permute-done.1, bf16[128,512]{1,0:T(8,128)(2,1)S(1)} %collective-permute-done, ...), kind=kOutput, calls=%fused_computation.11 | convolution fusion | flops 2164256768 | bytes 13221888 | tf_op jit(solution)/shard_map/thk,kj->thj/dot_general | solution.py:52
  59.4 10.1 %fusion.6 = (bf16[128,32,512]{0,2,1:T(8,128)(2,1)S(1)}, f32[512,128,32]{1,0,2:T(8,128)}) fusion(f32[128,32]{0,1:T(8,128)S(1)} %multiply_reduce_fusion, f32[128,32]{0,1:T(8,128)S(1)} %fusion.9, f32[128,32]{0,1:T(8,128)S(1)} %get-tuple-element.21, f32[512,128,32]{1,0,2:T(8,128)S(1)} %get-tuple-element.22, pred[128,512]{0,1:T(8,128)(4,1)S(1)} %fusion.34, ...), kind=kOutput, calls=%fused_computation.9 | convolution fusion | flops 2164260864 | bytes 25804800 | tf_op jit(solution)/shard_map/thj,kj->thk/dot_general | solution.py:54
  69.6 2.0 %copy-done.2 = bf16[128,32,512]{0,2,1:T(8,128)(2,1)} copy-done((bf16[128,32,512]{0,2,1:T(8,128)(2,1)}, bf16[128,32,512]{0,2,1:T(8,128)(2,1)S(1)}, u32[]{:S(2)}) %copy-start.2) | copy-done | bytes 4194328
  71.6 8.3 %fusion.30 = f32[512,512]{1,0:T(8,128)} fusion(f32[512,512]{1,0:T(8,128)S(1)} %fusion.22, bf16[128,32,512]{0,2,1:T(8,128)(2,1)S(1)} %get-tuple-element.23, bf16[128,32,512]{2,1,0:T(8,128)(2,1)} %param.7), kind=kOutput, calls=%fused_computation.30 | convolution fusion | flops 2147745792 | bytes 10485760 | tf_op jit(solution)/shard_map/thk,thj->kj/dot_general | solution.py:61
  80.2 8.6 %fusion.2 = bf16[512,32,128]{2,0,1:T(8,128)(2,1)} fusion(f32[512,128,32]{1,0,2:T(8,128)} %get-tuple-element.24, f32[512,128,32]{1,0,2:T(8,128)} %copy-done.1, f32[32,128]{1,0:T(8,128)S(1)} %bitcast.120, f32[32,128]{1,0:T(8,128)S(1)} %bitcast.119, f32[32,128]{1,0:T(8,128)S(1)} %bitcast.118, pred[512,128]{1,0:T(8,128)(4,1)S(1)} %fusion.36), kind=kLoop, calls=%fused_computation.3 | loop fusion | flops 14680064 | bytes 21086208 | tf_op jit(solution)/shard_map/convert_element_type | solution.py:55
  88.8 19.6 %reduce-scatter.4.cloned.1.call-done = f32[4,32,512]{2,1,0:T(8,128)} async-done(((f32[4,128,512]{2,1,0:T(8,128)}), f32[4,32,512]{2,1,0:T(8,128)}) %reduce-scatter.4.cloned.1.call-update) | async-done | bytes 262160 | tf_op jit(solution)/shard_map/reduce_scatter | solution.py:68
  109.2 1.3 collective-permute-start.6
  110.5 1.3 collective-permute-start.7
  111.8 1.3 collective-permute-start.8
  113.1 4.1 %convolution_bitcast_fusion = f32[4,128,64]{2,1,0:T(8,128)} fusion(bf16[4,128,32,128]{3,1,0,2:T(8,128)(2,1)} %bitcast.113, bf16[128,32,64,1]{0,2,3,1:T(8,128)(2,1)S(1)} %bitcast.115), kind=kOutput, calls=%fused_computation.32 | convolution fusion | flops 268435456 | bytes 4849664 | tf_op jit(solution)/shard_map/thk,thr->kr/dot_general | solution.py:64
  117.4 1.4 collective-permute-done.8
  119.7 8.4 %all_gather.6 = bf16[128,512]{1,0:T(8,128)(2,1)S(1)} all-gather(bf16[32,512]{1,0:T(8,128)(2,1)S(1)} %fusion.40), channel_id=1, replica_groups=mesh['ctx'=8,'head'=4] {'head'}, dimensions={0}, use_global_device_ids=true | all-gather | bytes 163840 | tf_op jit(solution)/shard_map/all_gather | solution.py:80
  128.1 2.5 %fusion.50 = f32[512,1792]{1,0:T(8,128)} fusion(bf16[128,512]{1,0:T(8,128)(2,1)S(1)} %all_gather.6, bf16[128,1792]{1,0:T(8,128)(2,1)S(1)} %copy-done), kind=kOutput, calls=%fused_computation.64 | convolution fusion | flops 234881024 | bytes 4259840 | tf_op jit(solution)/shard_map/dot_general | solution.py:84
  130.6 6.5 %convolution_convert_fusion = bf16[128,32,512]{2,0,1:T(8,128)(2,1)} fusion(bf16[128,32,512]{0,2,1:T(8,128)(2,1)} %copy-done.2, bf16[128,512]{1,0:T(8,128)(2,1)S(1)} %copy-done.3, bf16[128,512]{1,0:T(8,128)(2,1)S(1)} %collective-permute-done.2, bf16[128,512]{1,0:T(8,128)(2,1)S(1)} %collective-permute-done.1, bf16[128,512]{1,0:T(8,128)(2,1)S(1)} %collective-permute-done), kind=kOutput, calls=%fused_computation.25 | convolution fusion | flops 2151677952 | bytes 8912896 | tf_op jit(solution)/shard_map/thk,kj->thj/dot_general | solution.py:56
  137.1 7.4 %reduce-scatter.6.cloned.1.call-done = f32[4,32,64]{2,1,0:T(8,128)} async-done(((f32[4,128,64]{2,1,0:T(8,128)}), f32[4,32,64]{2,1,0:T(8,128)}) %reduce-scatter.6.cloned.1.call-update) | async-done | bytes 32784 | tf_op jit(solution)/shard_map/reduce_scatter | solution.py:69
  147.9 1.6 collective-permute-start.9
  149.5 3.0 %convolution_convert_fusion.1 = bf16[128,32,64]{0,2,1:T(8,128)(2,1)S(1)} fusion(bf16[128,32,512]{0,2,1:T(8,128)(2,1)} %copy-done.2, bf16[128,64]{0,1:T(8,128)(2,1)S(1)} %copy-done.4, bf16[128,64]{0,1:T(8,128)(2,1)S(1)} %collective-permute-done.5, bf16[128,64]{0,1:T(8,128)(2,1)S(1)} %collective-permute-done.4, bf16[128,64]{0,1:T(8,128)(2,1)S(1)} %collective-permute-done.3), kind=kOutput, calls=%fused_computation.31 | convolution fusion | flops 268959744 | bytes 4784128 | tf_op jit(solution)/shard_map/thk,kr->thr/dot_general | solution.py:59
  152.5 6.9 %copy.36 = bf16[128,32,512]{2,1,0:T(8,128)(2,1)} copy(bf16[128,32,512]{2,0,1:T(8,128)(2,1)} %convolution_convert_fusion) | data formatting | bytes 8388608
  161.1 8.2 %all_gather.7 = bf16[128,64]{1,0:T(8,128)(2,1)S(1)} all-gather(bf16[32,64]{1,0:T(8,128)(2,1)S(1)} %fusion.45), channel_id=1, replica_groups=mesh['ctx'=8,'head'=4] {'head'}, dimensions={0}, use_global_device_ids=true | all-gather | bytes 20480 | tf_op jit(solution)/shard_map/all_gather | solution.py:81
  170.0 22.7 %reduce-scatter.8.cloned.1.call-done = f32[64,1792]{1,0:T(8,128)} async-done(((f32[512,1792]{1,0:T(8,128)}), f32[64,1792]{1,0:T(8,128)}) %reduce-scatter.8.cloned.1.call-update) | async-done | bytes 458768 | tf_op jit(solution)/shard_map/reduce_scatter | solution.py:83
  (40 shorter events, 10.4 us)
Async XLA Ops:
  7.2 120.9 %copy-start = (bf16[128,1792]{1,0:T(8,128)(2,1)S(1)}, bf16[128,1792]{1,0:T(8,128)(2,1)}, u32[]{:S(2)}) copy-start(bf16[128,1792]{1,0:T(8,128)(2,1)} %param.12) | copy-start | bytes 1376260
  7.2 22.3 %copy-start.3 = (bf16[128,512]{1,0:T(8,128)(2,1)S(1)}, bf16[128,512]{1,0:T(8,128)(2,1)}, u32[]{:S(2)}) copy-start(bf16[128,512]{1,0:T(8,128)(2,1)} %param.9) | copy-start | bytes 393220
  7.2 101.1 %reduce-scatter.4.cloned.1.call-start = ((), (), s32[]{:S(2)}) async-start(), calls=%async_computation.3 | async-start | bytes 1310720 | tf_op jit(solution)/shard_map/reduce_scatter | solution.py:68
  7.2 18.0 %collective-permute-start.3 = (bf16[128,64]{0,1:T(8,128)(2,1)}, bf16[128,64]{0,1:T(8,128)(2,1)S(1)}, u32[]{:S(2)}, u32[]{:S(2)}) collective-permute-start(bf16[128,64]{0,1:T(8,128)(2,1)} %param.10), channel_id=1, source_target_pairs={{0,12},{4,16},{8,20},{12,24},{16,28},{1,13},{5,17},{9,21},{13,25},... | collective-permute-start | bytes 49160 | tf_op jit(solution)/shard_map/ppermute | solution.py:15
  11.8 15.7 %collective-permute-start.4 = (bf16[128,64]{0,1:T(8,128)(2,1)}, bf16[128,64]{0,1:T(8,128)(2,1)S(1)}, u32[]{:S(2)}, u32[]{:S(2)}) collective-permute-start(bf16[128,64]{0,1:T(8,128)(2,1)} %param.10), channel_id=1, source_target_pairs={{0,8},{4,12},{8,16},{12,20},{16,24},{20,28},{1,9},{5,13},{9,17},{1... | collective-permute-start | bytes 49160 | tf_op jit(solution)/shard_map/ppermute | solution.py:15
  15.3 12.2 %collective-permute-start.5 = (bf16[128,64]{0,1:T(8,128)(2,1)}, bf16[128,64]{0,1:T(8,128)(2,1)S(1)}, u32[]{:S(2)}, u32[]{:S(2)}) collective-permute-start(bf16[128,64]{0,1:T(8,128)(2,1)} %param.10), channel_id=1, source_target_pairs={{0,4},{4,8},{8,12},{12,16},{16,20},{20,24},{24,28},{1,5},{5,9},{9,... | collective-permute-start | bytes 49160 | tf_op jit(solution)/shard_map/ppermute | solution.py:15
  18.6 10.9 %collective-permute-start = (bf16[128,512]{1,0:T(8,128)(2,1)}, bf16[128,512]{1,0:T(8,128)(2,1)S(1)}, u32[]{:S(2)}, u32[]{:S(2)}) collective-permute-start(bf16[128,512]{1,0:T(8,128)(2,1)} %param.9), channel_id=1, source_target_pairs={{0,12},{4,16},{8,20},{12,24},{16,28},{1,13},{5,17},{9,21},{13,25},... | collective-permute-start | bytes 393224 | tf_op jit(solution)/shard_map/ppermute | solution.py:15
  20.4 9.1 %collective-permute-start.1 = (bf16[128,512]{1,0:T(8,128)(2,1)}, bf16[128,512]{1,0:T(8,128)(2,1)S(1)}, u32[]{:S(2)}, u32[]{:S(2)}) collective-permute-start(bf16[128,512]{1,0:T(8,128)(2,1)} %param.9), channel_id=1, source_target_pairs={{0,8},{4,12},{8,16},{12,20},{16,24},{20,28},{1,9},{5,13},{9,17},{1... | collective-permute-start | bytes 393224 | tf_op jit(solution)/shard_map/ppermute | solution.py:15
  25.2 4.3 %collective-permute-start.2 = (bf16[128,512]{1,0:T(8,128)(2,1)}, bf16[128,512]{1,0:T(8,128)(2,1)S(1)}, u32[]{:S(2)}, u32[]{:S(2)}) collective-permute-start(bf16[128,512]{1,0:T(8,128)(2,1)} %param.9), channel_id=1, source_target_pairs={{0,4},{4,8},{8,12},{12,16},{16,20},{20,24},{24,28},{1,5},{5,9},{9,... | collective-permute-start | bytes 393224 | tf_op jit(solution)/shard_map/ppermute | solution.py:15
  39.1 20.3 %copy-start.1 = (f32[512,128,32]{1,0,2:T(8,128)}, f32[512,128,32]{1,0,2:T(8,128)S(1)}, u32[]{:S(2)}) copy-start(f32[512,128,32]{1,0,2:T(8,128)S(1)} %get-tuple-element.22) | copy-start | bytes 25165828
  39.1 5.2 %copy-start.5 = (bf16[128,32,512]{2,1,0:T(8,128)(2,1)S(1)}, bf16[128,32,512]{2,1,0:T(8,128)(2,1)}, u32[]{:S(2)}) copy-start(bf16[128,32,512]{2,1,0:T(8,128)(2,1)} %param.11) | copy-start | bytes 12582916
  69.5 2.0 %copy-start.2 = (bf16[128,32,512]{0,2,1:T(8,128)(2,1)}, bf16[128,32,512]{0,2,1:T(8,128)(2,1)S(1)}, u32[]{:S(2)}) copy-start(bf16[128,32,512]{0,2,1:T(8,128)(2,1)S(1)} %get-tuple-element.23) | copy-start | bytes 12582916
  79.9 64.6 %reduce-scatter.6.cloned.1.call-start = ((), (), s32[]{:S(2)}) async-start(), calls=%async_computation.4 | async-start | bytes 327680 | tf_op jit(solution)/shard_map/reduce_scatter | solution.py:69
  109.2 8.1 %collective-permute-start.6 = (f32[32,512]{1,0:T(8,128)S(1)}, f32[32,512]{1,0:T(8,128)S(1)}, u32[]{:S(2)}, u32[]{:S(2)}) collective-permute-start(f32[32,512]{1,0:T(8,128)S(1)} %get-tuple-element.15), channel_id=1, source_target_pairs={{4,0},{8,4},{12,8},{16,12},{20,16},{24,20},{28,24},{5,1},{9,5},{13... | collective-permute-start | bytes 196616 | tf_op jit(solution)/shard_map/ppermute | solution.py:15
  110.5 6.9 %collective-permute-start.7 = (f32[32,512]{1,0:T(8,128)S(1)}, f32[32,512]{1,0:T(8,128)S(1)}, u32[]{:S(2)}, u32[]{:S(2)}) collective-permute-start(f32[32,512]{1,0:T(8,128)S(1)} %get-tuple-element.17), channel_id=1, source_target_pairs={{8,0},{12,4},{16,8},{20,12},{24,16},{28,20},{9,1},{13,5},{17,9},{2... | collective-permute-start | bytes 196616 | tf_op jit(solution)/shard_map/ppermute | solution.py:15
  111.8 6.9 %collective-permute-start.8 = (f32[32,512]{1,0:T(8,128)S(1)}, f32[32,512]{1,0:T(8,128)S(1)}, u32[]{:S(2)}, u32[]{:S(2)}) collective-permute-start(f32[32,512]{1,0:T(8,128)S(1)} %get-tuple-element.16), channel_id=1, source_target_pairs={{12,0},{16,4},{20,8},{24,12},{28,16},{13,1},{17,5},{21,9},{25,13},... | collective-permute-start | bytes 196616 | tf_op jit(solution)/shard_map/ppermute | solution.py:15
  117.3 75.4 %reduce-scatter.8.cloned.1.call-start = ((), (), s32[]{:S(2)}) async-start(), calls=%async_computation.5 | async-start | bytes 4128768 | tf_op jit(solution)/shard_map/reduce_scatter | solution.py:83
  128.1 21.4 %copy-start.4 = (bf16[128,64]{0,1:T(8,128)(2,1)S(1)}, bf16[128,64]{0,1:T(8,128)(2,1)}, u32[]{:S(2)}) copy-start(bf16[128,64]{0,1:T(8,128)(2,1)} %param.10) | copy-start | bytes 49156
  145.3 15.1 %collective-permute-start.10 = (f32[32,64]{1,0:T(8,128)S(1)}, f32[32,64]{1,0:T(8,128)S(1)}, u32[]{:S(2)}, u32[]{:S(2)}) collective-permute-start(f32[32,64]{1,0:T(8,128)S(1)} %get-tuple-element.20), channel_id=1, source_target_pairs={{8,0},{12,4},{16,8},{20,12},{24,16},{28,20},{9,1},{13,5},{17,9},{2... | collective-permute-start | bytes 24584 | tf_op jit(solution)/shard_map/ppermute | solution.py:15
  146.6 13.8 %collective-permute-start.11 = (f32[32,64]{1,0:T(8,128)S(1)}, f32[32,64]{1,0:T(8,128)S(1)}, u32[]{:S(2)}, u32[]{:S(2)}) collective-permute-start(f32[32,64]{1,0:T(8,128)S(1)} %get-tuple-element.19), channel_id=1, source_target_pairs={{12,0},{16,4},{20,8},{24,12},{28,16},{13,1},{17,5},{21,9},{25,13},... | collective-permute-start | bytes 24584 | tf_op jit(solution)/shard_map/ppermute | solution.py:15
  147.9 12.5 %collective-permute-start.9 = (f32[32,64]{1,0:T(8,128)S(1)}, f32[32,64]{1,0:T(8,128)S(1)}, u32[]{:S(2)}, u32[]{:S(2)}) collective-permute-start(f32[32,64]{1,0:T(8,128)S(1)} %get-tuple-element.18), channel_id=1, source_target_pairs={{4,0},{8,4},{12,8},{16,12},{20,16},{24,20},{28,24},{5,1},{9,5},{13... | collective-permute-start | bytes 24584 | tf_op jit(solution)/shard_map/ppermute | solution.py:15
Sparse Core Ops, SparseCore 0:
  80.0 28.2 reduce-scatter.3
  117.4 27.0 reduce-scatter.5
  147.4 45.2 reduce-scatter.7
where the time goes:
time: 201 us; the launch traced here: 200 us
  matrix products  61.2 us (30%)
  waiting for transfers between devices  51.3 us (26%)
  starting transfers between devices  25.2 us (13%)
  local copies, waits for them, and re-layouts  18.6 us (9%)
  blocking collectives  16.6 us (8%)
  between operations  14 us (7%)
  other arithmetic  13 us (6%)
    ppermute x12, starting transfers between devices, passed_along(): return lax.ppermute(array, axis, pairs)  25.1 us
    reduce_scatter x1, waiting for transfers between devices, shards(): lax.psum_scatter(lax.dot_general(latent_grad, inputs, (((0,), (0,)), ((),...  22.7 us
    reduce_scatter x1, waiting for transfers between devices, shards(): lax.psum_scatter(blocks_lat, 'head', scatter_dimension=1, tiled=True)  19.6 us
    unnamed x17, local copies, waits for them, and re-layouts  16.2 us
    dot_general x1, matrix products, shards(): jnp.einsum('thj,kj->thk', out_grad, keys_lat, preferred_element_type=jnp....  10.1 us
    dot_general x1, matrix products, shards(): jnp.einsum('thj,kj->thk', q_latent, keys_lat, preferred_element_type=jnp....  9.59 us
    convert_element_type x1, other arithmetic, shards(): (probs * (dprob - delta[..., None]) * softmax_scale).astype(jnp.bfloat16)  8.59 us
    all_gather x1, blocking collectives, shards(): lax.all_gather(own_lat.astype(jnp.bfloat16), 'head', axis=0, tiled=True)  8.41 us
  transfers between devices with their start and end apart: 15, of which 5 were waited for; matrix products, arithmetic and copies ran while one was open for 20% of the time, Pallas kernels for 0%

commit v1 on v0

v1 whole, which is shorter than its diff:
```python
import functools

import jax
import jax.numpy as jnp
from jax import lax
from jax.experimental import pallas as pl
from jax.experimental.pallas import tpu as pltpu
from jax.sharding import PartitionSpec as P


WIN_BLK = 3
DOCS = 4
CHUNK = 16
PAIR = 2
LANES = 128
DOC_VALUES = 8

softmax_scale = 192.0 ** (-0.5)


def nt(a, b):
    return lax.dot_general(a, b, (((1,), (1,)), ((), ())), preferred_element_type=jnp.float32)


def nn(a, b):
    return lax.dot_general(a, b, (((1,), (0,)), ((), ())), preferred_element_type=jnp.float32)


def tn(a, b):
    return lax.dot_general(a, b, (((0,), (0,)), ((), ())), preferred_element_type=jnp.float32)


def pack_kernel(lat_ref, rope_ref, out_ref):
    lat = lat_ref.shape[1]
    out_ref[:, :lat] = lat_ref[...]
    out_ref[:, lat:] = rope_ref[...].astype(jnp.float32).T.astype(out_ref.dtype)


def score_step(begin, keys_ref, first_ref, q_ref, qr_ref, do_ref, ds_ref, acc_ref, turn_ref, *, width, lat, heads, window):
    keys = keys_ref[pl.ds(begin, width), :]
    klat = keys[:, :lat]
    q = q_ref[...]
    do = do_ref[...]
    block = q.shape[0]
    rope = turn_ref.shape[1]
    turned = qr_ref[...].astype(jnp.float32)
    for head in range(heads):
        turn_ref[pl.ds(head, CHUNK, stride=heads), :] = turned[:, head * rope:(head + 1) * rope]
    qr = turn_ref[...].astype(jnp.bfloat16)
    firsts = []
    lasts = []
    for at in range(0, block, LANES):
        token = begin + (lax.broadcasted_iota(jnp.int32, first_ref.shape, 1) + at) // heads
        firsts.append(jnp.take_along_axis(first_ref[...], token, axis=1, mode="promise_in_bounds")[:1])
        lasts.append(token[:1] + window)
    first = jnp.concatenate(firsts, axis=1)
    last = jnp.concatenate(lasts, axis=1)
    scores = nt(klat, q) + nt(keys[:, lat:], qr)
    pos = lax.broadcasted_iota(jnp.int32, scores.shape, 0) + begin
    allowed = (pos >= first) & (pos <= last)
    scores = jnp.where(allowed, scores, -jnp.inf)
    top = jnp.max(scores, axis=0, keepdims=True)
    expo = jnp.exp((scores - top) * softmax_scale)
    inverse = 1.0 / jnp.sum(expo, axis=0, keepdims=True)
    probs = expo * inverse
    low = probs.astype(jnp.bfloat16)
    dprob = nt(klat, do)
    delta = jnp.sum(low.astype(jnp.float32) * dprob, axis=0, keepdims=True)
    ds = (probs * (dprob - delta) * softmax_scale).astype(jnp.bfloat16)
    ds_ref[0] = ds
    acc_ref[pl.ds(begin, width), :lat] += nn(ds, q) + nn(low, do)
    acc_ref[pl.ds(begin, width), lat:] += nn(ds, qr)


def score_kernel(place_ref, doc_ref, q_ref, qr_ref, do_ref, *refs, width, lat, heads, window):
    blocks, (ds_ref, keys_ref, acc_ref, first_ref, turn_ref) = refs[:-5], refs[-5:]
    tok = blocks[0].shape[0]
    step = pl.program_id(0)

    @pl.when(step == 0)
    def _():
        acc_ref[...] = jnp.zeros_like(acc_ref)
        for slot, packed in enumerate(blocks):
            keys_ref[slot * tok:(slot + 1) * tok, :] = packed[...]
        rank = place_ref[0]
        ids = doc_ref[...]
        mine = doc_ref[pl.ds(rank, 1), :]
        begins = jnp.zeros(mine.shape, jnp.float32)
        for value in range(DOC_VALUES - 1):
            count = jnp.sum(jnp.where(ids == value, 1.0, 0.0), axis=0, keepdims=True)
            count = jnp.sum(count, axis=1, keepdims=True)
            begins += jnp.where(mine > value, count, 0.0)
        here = lax.broadcasted_iota(jnp.int32, mine.shape, 1) + rank * tok
        first = jnp.maximum(begins.astype(jnp.int32), here - (window - 1)) - (rank * tok - window)
        first_ref[...] = jnp.broadcast_to(first, first_ref.shape)

    begin = pl.multiple_of(step * CHUNK, CHUNK)
    score_step(begin, keys_ref, first_ref, q_ref, qr_ref, do_ref, ds_ref, acc_ref, turn_ref,
               width=width, lat=lat, heads=heads, window=window)


def score_more_kernel(first_ref, q_ref, qr_ref, do_ref, keys_ref, had_ref, *refs, width, lat, heads, window, offset):
    ds_ref, part_refs, acc_ref, turn_ref = refs[0], refs[1:-2], refs[-2], refs[-1]
    step = pl.program_id(0)

    @pl.when(step == 0)
    def _():
        acc_ref[...] = had_ref[...]

    begin = pl.multiple_of((step + offset) * CHUNK, CHUNK)
    score_step(begin, keys_ref, first_ref, q_ref, qr_ref, do_ref, ds_ref, acc_ref, turn_ref,
               width=width, lat=lat, heads=heads, window=window)

    @pl.when(step == pl.num_programs(0) - 1)
    def _():
        for slot, part_ref in enumerate(part_refs):
            tok = part_ref.shape[0]
            part_ref[...] = acc_ref[slot * tok:(slot + 1) * tok, :].astype(part_ref.dtype)


def query_kernel(ds_ref, keys_ref, *refs, width, lat, heads, offset):
    dq_ref, dqr_ref, turn_ref = refs[-3:]
    begin = pl.multiple_of((pl.program_id(0) + offset) * CHUNK, CHUNK)
    keys = keys_ref[pl.ds(begin, width), :]
    ds = ds_ref[0]
    dq_ref[...] = tn(ds, keys[:, :lat]).astype(dq_ref.dtype)
    turn_ref[...] = tn(ds, keys[:, lat:])
    rope = turn_ref.shape[1]
    for head in range(0, heads, 2):
        pair = [turn_ref[pl.ds(head + which, CHUNK, stride=heads), :] for which in range(2)]
        dqr_ref[:, head * rope:(head + 2) * rope] = jnp.concatenate(pair, axis=1).astype(dqr_ref.dtype)


def proj_kernel(place_ref, index_ref, *refs, groups):
    pieces, fed, out_ref, all_ref = refs[:groups], refs[groups:-2], refs[-2], refs[-1]
    half = out_ref.shape[1]
    all_ref[groups] = jnp.zeros(all_ref.shape[1:], all_ref.dtype)
    for by, piece in enumerate(pieces):
        all_ref[(place_ref[1] - by + groups) % groups] = piece[...]
    lefts = [all_ref[index_ref[k]] for k in range(len(fed))]
    span = out_ref.shape[2]
    for at in range(0, span, 2 * LANES):
        lanes = slice(at, min(at + 2 * LANES, span))
        product = tn(lefts[0], fed[0][:, lanes])
        for left, right in zip(lefts[1:], fed[1:]):
            product += tn(left, right[:, lanes])
        for core in range(PAIR):
            out_ref[place_ref[0] ^ core, :, lanes] = product[core * half:(core + 1) * half]


def ring(peers, by):
    return [(i, (i + by) % peers) for i in range(peers)]


def line(groups, stage, edge):
    pairs = []
    for left in range(edge, groups - 1, 2):
        if left + 1 - stage >= 0:
            pairs.append((left, left + 1))
        if left + stage < groups:
            pairs.append((left + 1, left))
    return pairs


def across(peers, by):
    return [(i, i ^ by) for i in range(peers)]


def stride_ring(peers, by):
    return [(i, (i + PAIR * by) % peers) for i in range(peers)]


def in_hbm(array):
    return pltpu.with_memory_space_constraint(array, pltpu.HBM)


def shards(q_latent, q_rope, latent, key_rope, out_grad, inputs, doc_ids):
    tok, heads, lat = q_latent.shape
    rope = key_rope.shape[1]
    total = doc_ids.shape[0]
    ctxs = lax.axis_size("ctx")
    headers = lax.axis_size("head")
    window = min(WIN_BLK * tok, total // DOCS)
    depth = window // tok
    slots = depth + 1
    rank = lax.axis_index("ctx")
    rows = tok * heads
    steps = tok // CHUNK
    block = CHUNK * heads
    keyed = lat + rope
    groups = ctxs // PAIR
    low = jnp.bfloat16
    smem = pl.BlockSpec(memory_space=pltpu.SMEM)
    whole_of = pl.BlockSpec(memory_space=pltpu.VMEM)

    packed = pl.pallas_call(
        pack_kernel,
        in_specs=[whole_of, whole_of],
        out_specs=whole_of,
        out_shape=jax.ShapeDtypeStruct((tok, keyed), low),
        name="pack",
    )(latent, key_rope.T)
    earlier = [lax.ppermute(packed, "ctx", ring(ctxs, back)) for back in range(depth, 0, -1)]
    fed, source = [inputs], [rank // PAIR]
    flows = [inputs, inputs]
    for stage in range(1, groups):
        moved = []
        for edge in range(2):
            pairs = line(groups, stage, edge)
            if not pairs:
                moved.append(None)
                continue
            moved.append(lax.ppermute(flows[1 - edge], "ctx", [(PAIR * a + c, PAIR * b + c) for a, b in pairs for c in range(PAIR)]))
            fed.append(moved[edge])
            ahead = (rank // PAIR) % 2 == edge
            origin = rank // PAIR + jnp.where(ahead, stage, -stage)
            source.append(jnp.where((origin >= 0) & (origin < groups), origin, groups))
        flows = moved

    q = q_latent.reshape(rows, lat)
    do = out_grad.reshape(rows, lat)
    span = window + tok
    width = window + CHUNK
    places = rank.astype(jnp.int32).reshape(1)
    split = steps // 2
    resident = lambda *shape: pl.BlockSpec(shape, lambda i: (0,) * len(shape))
    limits = pltpu.CompilerParams(dimension_semantics=("arbitrary",), vmem_limit_bytes=32 * 1024 * 1024)
    sizes = dict(width=width, lat=lat, heads=heads, window=window)
    cost = pl.CostEstimate(flops=rows * width * (5 * lat), transcendentals=0, bytes_accessed=6 << 20)

    def tiles(offset):
        return [
            pl.BlockSpec((block, lat), lambda i: (i + offset, 0)),
            pl.BlockSpec((CHUNK, heads * rope), lambda i: (i + offset, 0)),
            pl.BlockSpec((block, lat), lambda i: (i + offset, 0)),
        ]

    chunk_of = pl.BlockSpec((1, width, block), lambda i: (i, 0, 0))
    ds_shape = jax.ShapeDtypeStruct((split, width, block), low)
    turner = pltpu.VMEM((block, rope), jnp.float32)
    streams = (in_hbm(q), in_hbm(q_rope), in_hbm(do))
    ds0, keys, acc, first = pl.pallas_call(
        functools.partial(score_kernel, **sizes),
        grid=(split,),
        in_specs=[smem, resident(ctxs, tok)] + tiles(0) + [resident(tok, keyed)] * slots,
        out_specs=[chunk_of, resident(span, keyed), resident(span, keyed), resident(8, tok)],
        out_shape=[
            ds_shape,
            jax.ShapeDtypeStruct((span, keyed), low),
            jax.ShapeDtypeStruct((span, keyed), jnp.float32),
            jax.ShapeDtypeStruct((8, tok), jnp.int32),
        ],
        scratch_shapes=[turner],
        compiler_params=limits,
        cost_estimate=cost,
        name="score0",
    )(places, doc_ids.reshape(ctxs, tok), *streams, *earlier, packed)
    ds1, *part = pl.pallas_call(
        functools.partial(score_more_kernel, offset=split, **sizes),
        grid=(split,),
        in_specs=[resident(8, tok)] + tiles(split) + [resident(span, keyed)] * 2,
        out_specs=[chunk_of] + [resident(tok, keyed)] * slots,
        out_shape=[ds_shape] + [jax.ShapeDtypeStruct((tok, keyed), low)] * depth
        + [jax.ShapeDtypeStruct((tok, keyed), jnp.float32)],
        scratch_shapes=[pltpu.VMEM((span, keyed), jnp.float32), turner],
        compiler_params=limits,
        cost_estimate=cost,
        name="score1",
    )(first, *streams, keys, acc)

    shapes = [jax.ShapeDtypeStruct((rows, lat), low), jax.ShapeDtypeStruct((tok, heads * rope), low)]
    grads = ()
    for call, ds in enumerate((ds0, ds1)):
        offset = call * split
        grads = pl.pallas_call(
            functools.partial(query_kernel, width=width, lat=lat, heads=heads, offset=offset),
            grid=(split,),
            in_specs=[chunk_of, resident(span, keyed)] + [pl.BlockSpec(memory_space=pl.ANY)] * len(grads),
            out_specs=tiles(offset)[:2],
            out_shape=shapes,
            scratch_shapes=[turner],
            input_output_aliases={2: 0, 3: 1} if call else {},
            compiler_params=limits,
            cost_estimate=pl.CostEstimate(flops=rows * width * lat, transcendentals=0, bytes_accessed=4 << 20),
            name="query",
        )(ds, keys, *[in_hbm(grad) for grad in grads])
    q_latent_grad = grads[0].reshape(tok, heads, lat)
    q_rope_grad = grads[1]

    mine = part[depth]
    for back in range(1, depth + 1):
        mine = mine + lax.ppermute(part[depth - back], "ctx", ring(ctxs, -back)).astype(jnp.float32)
    sent = mine.astype(low)
    whole = mine
    for by in range(1, headers):
        whole = whole + lax.ppermute(sent, "head", across(headers, by)).astype(jnp.float32)
    found = whole.astype(low)
    latent_grad = found[:, :lat]
    key_rope_grad = found[:, lat:]

    narrow = PAIR * lat // ctxs
    mine_at = rank // PAIR
    pieces = []
    for by in range(groups):
        piece = lax.dynamic_slice_in_dim(found, ((mine_at + by) % groups) * narrow, narrow, 1)
        pieces.append(lax.ppermute(piece, "ctx", stride_ring(ctxs, by)) if by else piece)
    words = jnp.stack([rank % PAIR, mine_at]).astype(jnp.int32)
    width_in = inputs.shape[1]
    product = pl.pallas_call(
        functools.partial(proj_kernel, groups=groups),
        in_specs=[smem, smem] + [whole_of] * (groups + len(fed)),
        out_specs=whole_of,
        out_shape=jax.ShapeDtypeStruct((PAIR, lat // ctxs, width_in), jnp.float32),
        scratch_shapes=[pltpu.VMEM((groups + 1, tok, narrow), low)],
        compiler_params=pltpu.CompilerParams(vmem_limit_bytes=24 * 1024 * 1024),
        name="proj",
    )(words, jnp.stack(source).astype(jnp.int32), *pieces, *fed)
    proj_grad = product[0] + lax.ppermute(product[1], "ctx", across(ctxs, 1))
    return (q_latent_grad, q_rope_grad, latent_grad, key_rope_grad, proj_grad)


def solution(mesh):
    placed = (
        P("ctx", "head", None),
        P("ctx", "head"),
        P("ctx", None),
        P("ctx", None),
        P("ctx", "head", None),
        P("ctx", "head"),
        P(),
    )

    return jax.shard_map(
        shards,
        mesh=mesh,
        in_specs=placed,
        out_specs=(
            P("ctx", "head", None),
            P("ctx", "head"),
            P("ctx", None),
            P("ctx", None),
            P("ctx", "head"),
        ),
        check_vma=False,
    )
```

time: 201 us -> 90.2 us (0.45)
  matrix products: 61.2 us -> 0 us
  waiting for transfers between devices: 51.3 us -> 19.8 us
  Pallas kernels: 0 us -> 24.2 us
  blocking collectives: 16.6 us -> 0 us
  between operations: 14 us -> 0.81 us
  local copies, waits for them, and re-layouts: 18.6 us -> 6.62 us
  starting transfers between devices: 25.2 us -> 34.2 us
  other arithmetic: 13 us -> 4 us
    dot_general x10 -> x0, matrix products: 61.2 us -> none  [the longest x1 10.1 us: shards(): jnp.einsum('thj,kj->thk', out_grad, keys_lat, preferred_element_type=jnp....]
    reduce_scatter x3 -> x0, waiting for transfers between devices: 49.7 us -> none  [the longest x1 22.7 us: shards(): lax.psum_scatter(lax.dot_general(latent_grad, inputs, (((0,), (0,)), ((),...]
    pallas_call x0 -> x6, Pallas kernels: none -> 24.2 us  [the longest x2 7.25 us: shards(): pl.pallas_call(functools.partial(query_kernel, width=width, lat=lat, head...]
    ppermute x12 -> x16, waiting for transfers between devices: 1.47 us -> 19.8 us  [the longest x3 6.44 us: shards(): lax.ppermute(piece, 'ctx', stride_ring(ctxs, by))]
    all_gather x2 -> x0, blocking collectives: 16.6 us -> none  [the longest x1 8.41 us: shards(): lax.all_gather(own_lat.astype(jnp.bfloat16), 'head', axis=0, tiled=True)]
    unnamed x17 -> x27, local copies, waits for them, and re-layouts: 16.2 us -> 5.7 us
    ppermute x12 -> x16, starting transfers between devices: 25.1 us -> 34.2 us  [the longest x3 17.3 us: shards(): lax.ppermute(piece, 'ctx', stride_ring(ctxs, by))]
    convert_element_type x3 -> x2, other arithmetic: 10.2 us -> 2.09 us  [the longest x1 1.35 us: shards(): found = whole.astype(low)]
  transfers between devices with their start and end apart: 15 -> 16, of which waited for: 5 -> 8; matrix products, arithmetic and copies ran while one was open for 20% -> 4% of each run, Pallas kernels for 0% -> 23%
where the time goes in v1:
time: 90.2 us; the launch traced here: 89.7 us
  starting transfers between devices  34.2 us (38%)
  Pallas kernels  24.2 us (27%)
  waiting for transfers between devices  19.8 us (22%)
  local copies, waits for them, and re-layouts  6.62 us (7%)
  other arithmetic  4 us (4%)
    ppermute x3, starting transfers between devices, shards(): lax.ppermute(piece, 'ctx', stride_ring(ctxs, by))  17.3 us
    pallas_call x2, Pallas kernels, shards(): pl.pallas_call(functools.partial(query_kernel, width=width, lat=lat, head...  7.25 us
    pallas_call x1, Pallas kernels, shards(): pl.pallas_call(functools.partial(score_more_kernel, offset=split, **sizes...  6.53 us
    pallas_call x1, Pallas kernels, shards(): pl.pallas_call(functools.partial(score_kernel, **sizes), grid=(split,), i...  6.44 us
    ppermute x3, waiting for transfers between devices, shards(): lax.ppermute(piece, 'ctx', stride_ring(ctxs, by))  6.44 us
    ppermute x5, starting transfers between devices, shards(): lax.ppermute(flows[1 - edge], 'ctx', [(PAIR * a + c, PAIR * b + c) for a,...  6.27 us
    ppermute x2, waiting for transfers between devices, shards(): lax.ppermute(packed, 'ctx', ring(ctxs, back))  5.81 us
    unnamed x27, local copies, waits for them, and re-layouts  5.7 us
  transfers between devices with their start and end apart: 16, of which 8 were waited for; matrix products, arithmetic and copies ran while one was open for 4% of the time, Pallas kernels for 23%

profile of v1, /device:TPU:0, one launch (start us, length us, event | category | flops | bytes accessed | tf_op | source)
XLA Modules:
  0.0 89.7 jit_solution(17642603807544064791)
XLA Ops:
  0.6 1.7 %pack.1.refs_2_ = bf16[128,576]{1,0:T(8,128)(2,1)} custom-call(bf16[128,512]{1,0:T(8,128)(2,1)} %lat_ref.1, bf16[64,128]{1,0:T(8,128)(2,1)} %bitcast.21), custom_call_target="tpu_custom_call" | custom-call | tf_op jit(solution)/shard_map/pack/pallas_call | solution.py:196
  2.8 2.6 %collective-permute-start = (bf16[128,576]{1,0:T(8,128)(2,1)}, bf16[128,576]{1,0:T(8,128)(2,1)S(1)}, u32[]{:S(2)}, u32[]{:S(2)}) collective-permute-start(bf16[128,576]{1,0:T(8,128)(2,1)} %pack.1.refs_2_), channel_id=1, source_target_pairs={{0,8},{4,12},{8,16},{12,20},{16,24},{20,28},{24,0},{28,4},{1,9},{5... | collective-permute-start | bytes 442376 | tf_op jit(solution)/shard_map/ppermute | solution.py:203
  5.4 1.6 %collective-permute-start.10 = (bf16[128,1792]{1,0:T(8,128)(2,1)}, bf16[128,1792]{1,0:T(8,128)(2,1)S(1)}, u32[]{:S(2)}, u32[]{:S(2)}) collective-permute-start(bf16[128,1792]{1,0:T(8,128)(2,1)} %refs_4_.1), channel_id=1, source_target_pairs={{0,8},{4,12},{8,0},{12,4},{16,24},{20,28},{24,16},{28,20},{1,9},{5... | collective-permute-start | bytes 1376264 | tf_op jit(solution)/shard_map/ppermute | solution.py:213
  6.9 4.1 %collective-permute-done.1.refs_1_ = bf16[128,576]{1,0:T(8,128)(2,1)S(1)} collective-permute-done((bf16[128,576]{1,0:T(8,128)(2,1)}, bf16[128,576]{1,0:T(8,128)(2,1)S(1)}, u32[]{:S(2)}, u32[]{:S(2)}) %collective-permute-start.1) | collective-permute-done | bytes 147488 | tf_op jit(solution)/shard_map/ppermute | solution.py:203
  11.0 1.7 %collective-permute-done.refs_0_ = bf16[128,576]{1,0:T(8,128)(2,1)S(1)} collective-permute-done((bf16[128,576]{1,0:T(8,128)(2,1)}, bf16[128,576]{1,0:T(8,128)(2,1)S(1)}, u32[]{:S(2)}, u32[]{:S(2)}) %collective-permute-start) | collective-permute-done | bytes 147488 | tf_op jit(solution)/shard_map/ppermute | solution.py:203
  12.7 0.9 %copy-done.3 = bf16[128,576]{1,0:T(8,128)(2,1)S(1)} copy-done((bf16[128,576]{1,0:T(8,128)(2,1)S(1)}, bf16[128,576]{1,0:T(8,128)(2,1)}, u32[]{:S(2)}) %copy-start.3) | copy-done | bytes 147480
  13.7 0.7 copy-done.6
  14.3 6.4 %score0.1 = (bf16[4,272,512]{2,1,0:T(8,128)(2,1)S(1)}, bf16[384,576]{1,0:T(8,128)(2,1)S(1)}, f32[384,576]{1,0:T(8,128)S(1)}, s32[8,128]{1,0:T(8,128)S(1)}) custom-call(s32[1]{0:T(128)} %bitcast.place_ref, s32[8,128]{1,0:T(8,128)S(1)} %bitcast.19, bf16[4096,512]{1,0:T(8,128)(2,1)} %bitcast.22, bf16[128,2048]{1,0:T(8,128)(2,1)} %qr_ref.3, ...), custom_call_target="tpu_custom_call" | custom-call | flops 2852126720 | bytes 6291456 | tf_op jit(solution)/shard_map/score0/pallas_call | solution.py:242
  20.8 1.0 %copy-done.7 = bf16[4,272,512]{2,1,0:T(8,128)(2,1)} copy-done((bf16[4,272,512]{2,1,0:T(8,128)(2,1)}, bf16[4,272,512]{2,1,0:T(8,128)(2,1)S(1)}, u32[]{:S(2)}) %copy-start.7) | copy-done | bytes 1114136
  21.8 6.5 %score1.1 = (bf16[4,272,512]{2,1,0:T(8,128)(2,1)S(1)}, bf16[128,576]{1,0:T(8,128)(2,1)S(1)}, bf16[128,576]{1,0:T(8,128)(2,1)S(1)}, f32[128,576]{1,0:T(8,128)S(1)}) custom-call(s32[8,128]{1,0:T(8,128)S(1)} %get-tuple-element.17.first_ref, bf16[4096,512]{1,0:T(8,128)(2,1)} %bitcast.23, bf16[128,2048]{1,0:T(8,128)(2,1)} %qr_ref.3, bf16[4096,512]{1,0:T(8,128)(2,1)} %bitcast.25, ...), custom_call_target="tpu_custom_call" | custom-call | flops 2852126720 | bytes 6291456 | tf_op jit(solution)/shard_map/score1/pallas_call | solution.py:258
  28.3 4.1 %collective-permute-start.2 = (bf16[128,576]{1,0:T(8,128)(2,1)S(1)}, bf16[128,576]{1,0:T(8,128)(2,1)S(1)}, u32[]{:S(2)}, u32[]{:S(2)}) collective-permute-start(bf16[128,576]{1,0:T(8,128)(2,1)S(1)} %get-tuple-element.27), channel_id=1, source_target_pairs={{0,28},{4,0},{8,4},{12,8},{16,12},{20,16},{24,20},{28,24},{1,29},{... | collective-permute-start | bytes 442376 | tf_op jit(solution)/shard_map/ppermute | solution.py:292
  33.1 1.4 %collective-permute-start.13 = (bf16[128,1792]{1,0:T(8,128)(2,1)S(1)}, bf16[128,1792]{1,0:T(8,128)(2,1)}, u32[]{:S(2)}, u32[]{:S(2)}) collective-permute-start(bf16[128,1792]{1,0:T(8,128)(2,1)S(1)} %collective-permute-done.10.refs_5_), channel_id=1, source_target_pairs={{8,16},{12,20},{16,8},{20,12},{9,17},{13,21},{17,9},{21,13},{10,18... | collective-permute-start | bytes 1376264 | tf_op jit(solution)/shard_map/ppermute | solution.py:213
  34.5 2.0 %collective-permute-done.2 = bf16[128,576]{1,0:T(8,128)(2,1)S(1)} collective-permute-done((bf16[128,576]{1,0:T(8,128)(2,1)S(1)}, bf16[128,576]{1,0:T(8,128)(2,1)S(1)}, u32[]{:S(2)}, u32[]{:S(2)}) %collective-permute-start.2) | collective-permute-done | bytes 147488 | tf_op jit(solution)/shard_map/ppermute | solution.py:292
  36.5 1.8 %collective-permute-done.3 = bf16[128,576]{1,0:T(8,128)(2,1)S(1)} collective-permute-done((bf16[128,576]{1,0:T(8,128)(2,1)S(1)}, bf16[128,576]{1,0:T(8,128)(2,1)S(1)}, u32[]{:S(2)}, u32[]{:S(2)}) %collective-permute-start.3) | collective-permute-done | bytes 147488 | tf_op jit(solution)/shard_map/ppermute | solution.py:292
  38.3 0.7 fusion.1
  39.0 2.8 %collective-permute-start.6 = (bf16[128,576]{1,0:T(8,128)(2,1)}, bf16[128,576]{1,0:T(8,128)(2,1)}, u32[]{:S(2)}, u32[]{:S(2)}) collective-permute-start(bf16[128,576]{1,0:T(8,128)(2,1)} %fusion.1), channel_id=1, source_target_pairs={{0,3},{1,2},{2,1},{3,0},{4,7},{5,6},{6,5},{7,4},{8,11},{9,10},{10,... | collective-permute-start | bytes 442376 | tf_op jit(solution)/shard_map/ppermute | solution.py:296
  42.5 1.3 %collective-permute-start.12 = (bf16[128,1792]{1,0:T(8,128)(2,1)S(1)}, bf16[128,1792]{1,0:T(8,128)(2,1)}, u32[]{:S(2)}, u32[]{:S(2)}) collective-permute-start(bf16[128,1792]{1,0:T(8,128)(2,1)S(1)} %collective-permute-done.11.refs_6_), channel_id=1, source_target_pairs={{8,0},{12,4},{16,24},{20,28},{9,1},{13,5},{17,25},{21,29},{10,2},{... | collective-permute-start | bytes 1376264 | tf_op jit(solution)/shard_map/ppermute | solution.py:213
  43.8 1.3 %collective-permute-start.14 = (bf16[128,1792]{1,0:T(8,128)(2,1)}, bf16[128,1792]{1,0:T(8,128)(2,1)}, u32[]{:S(2)}, u32[]{:S(2)}) collective-permute-start(bf16[128,1792]{1,0:T(8,128)(2,1)} %collective-permute-done.13.refs_8_), channel_id=1, source_target_pairs={{8,0},{12,4},{16,24},{20,28},{9,1},{13,5},{17,25},{21,29},{10,2},{... | collective-permute-start | bytes 1376264 | tf_op jit(solution)/shard_map/ppermute | solution.py:213
  45.1 1.7 %collective-permute-done.6 = bf16[128,576]{1,0:T(8,128)(2,1)} collective-permute-done((bf16[128,576]{1,0:T(8,128)(2,1)}, bf16[128,576]{1,0:T(8,128)(2,1)}, u32[]{:S(2)}, u32[]{:S(2)}) %collective-permute-start.6) | collective-permute-done | bytes 147488 | tf_op jit(solution)/shard_map/ppermute | solution.py:296
  46.8 1.9 %collective-permute-done.5 = bf16[128,576]{1,0:T(8,128)(2,1)} collective-permute-done((bf16[128,576]{1,0:T(8,128)(2,1)}, bf16[128,576]{1,0:T(8,128)(2,1)}, u32[]{:S(2)}, u32[]{:S(2)}) %collective-permute-start.5) | collective-permute-done | bytes 147488 | tf_op jit(solution)/shard_map/ppermute | solution.py:296
  48.9 1.4 %add_convert_fusion = bf16[128,576]{1,0:T(8,128)(2,1)S(1)} fusion(bf16[128,576]{1,0:T(8,128)(2,1)} %collective-permute-done.6, bf16[128,576]{1,0:T(8,128)(2,1)} %collective-permute-done.5, bf16[128,576]{1,0:T(8,128)(2,1)} %collective-permute-done.4, bf16[128,576]{1,0:T(8,128)(2,1)} %copy-done.12, f32[128,576]{1,0:T(8,128)S(1)} %get-tuple-element.26, ...), kind=kLoop, calls=%fused_computation.3 | loop fusion | flops 811008 | bytes 1179648 | tf_op jit(solution)/shard_map/convert_element_type | solution.py:297
  50.5 4.1 %collective-permute-start.9 = (bf16[128,128]{1,0:T(8,128)(2,1)S(1)}, bf16[128,128]{1,0:T(8,128)(2,1)S(1)}, u32[]{:S(2)}, u32[]{:S(2)}) collective-permute-start(bf16[128,128]{1,0:T(8,128)(2,1)S(1)} %get-tuple-element.34), channel_id=1, source_target_pairs={{0,24},{4,28},{8,0},{12,4},{16,8},{20,12},{24,16},{28,20},{1,25},{... | collective-permute-start | bytes 98312 | tf_op jit(solution)/shard_map/ppermute | solution.py:306
  54.5 11.3 %collective-permute-start.8 = (bf16[128,128]{1,0:T(8,128)(2,1)S(1)}, bf16[128,128]{1,0:T(8,128)(2,1)S(1)}, u32[]{:S(2)}, u32[]{:S(2)}) collective-permute-start(bf16[128,128]{1,0:T(8,128)(2,1)S(1)} %get-tuple-element.35), channel_id=1, source_target_pairs={{0,16},{4,20},{8,24},{12,28},{16,0},{20,4},{24,8},{28,12},{1,17},{... | collective-permute-start | bytes 98312 | tf_op jit(solution)/shard_map/ppermute | solution.py:306
  65.8 1.9 %collective-permute-start.7 = (bf16[128,128]{1,0:T(8,128)(2,1)S(1)}, bf16[128,128]{1,0:T(8,128)(2,1)S(1)}, u32[]{:S(2)}, u32[]{:S(2)}) collective-permute-start(bf16[128,128]{1,0:T(8,128)(2,1)S(1)} %get-tuple-element.36), channel_id=1, source_target_pairs={{0,8},{4,12},{8,16},{12,20},{16,24},{20,28},{24,0},{28,4},{1,9},{5... | collective-permute-start | bytes 98312 | tf_op jit(solution)/shard_map/ppermute | solution.py:306
  67.9 6.4 %collective-permute-done.9.refs_3_ = bf16[128,128]{1,0:T(8,128)(2,1)S(1)} collective-permute-done((bf16[128,128]{1,0:T(8,128)(2,1)S(1)}, bf16[128,128]{1,0:T(8,128)(2,1)S(1)}, u32[]{:S(2)}, u32[]{:S(2)}) %collective-permute-start.9) | collective-permute-done | bytes 32800 | tf_op jit(solution)/shard_map/ppermute | solution.py:306
  75.0 1.0 %copy-done.2 = bf16[128,1792]{1,0:T(8,128)(2,1)S(1)} copy-done((bf16[128,1792]{1,0:T(8,128)(2,1)S(1)}, bf16[128,1792]{1,0:T(8,128)(2,1)}, u32[]{:S(2)}) %copy-start.2) | copy-done | bytes 458776
  76.0 0.8 copy-done.5
  76.8 2.3 %proj.1 = f32[2,64,1792]{2,1,0:T(8,128)S(1)} custom-call(s32[2]{0:T(128)S(1)} %pad_add_fusion.place_ref, s32[6]{0:T(128)S(1)} %stack.36.index_ref, bf16[128,128]{1,0:T(8,128)(2,1)S(1)} %get-tuple-element.37.refs_0_, bf16[128,128]{1,0:T(8,128)(2,1)S(1)} %copy-done.5, bf16[128,128]{1,0:T(8,128)(2,1)S(1)} %collective-permute-done.8.refs_2_, ...), custom_call_target="tpu_custom_call" | custom-call | tf_op jit(solution)/shard_map/proj/pallas_call | solution.py:309
  79.2 3.6 %query.2 = (bf16[4096,512]{1,0:T(8,128)(2,1)}, bf16[128,2048]{1,0:T(8,128)(2,1)}) custom-call(bf16[4,272,512]{2,1,0:T(8,128)(2,1)S(1)} %copy-done.8, bf16[384,576]{1,0:T(8,128)(2,1)S(1)} %get-tuple-element.18.keys_ref), custom_call_target="tpu_custom_call" | custom-call | flops 570425344 | bytes 4194304 | tf_op jit(solution)/shard_map/query/pallas_call | solution.py:275
  82.9 3.6 %query.3 = (bf16[4096,512]{1,0:T(8,128)(2,1)}, bf16[128,2048]{1,0:T(8,128)(2,1)}) custom-call(bf16[4,272,512]{2,1,0:T(8,128)(2,1)S(1)} %get-tuple-element.20.ds_ref, bf16[384,576]{1,0:T(8,128)(2,1)S(1)} %get-tuple-element.18.keys_ref, bf16[4096,512]{1,0:T(8,128)(2,1)} %get-tuple-element.22.refs_0_, ...), custom_call_target="tpu_custom_call", output_to_operand_aliasing={{0}: (2, {}), {1}: (3, {})} | custom-call | flops 570425344 | bytes 4194304 | tf_op jit(solution)/shard_map/query/pallas_call | solution.py:275
  87.2 0.7 copy.14
  87.9 1.8 %fusion = f32[64,1792]{1,0:T(8,128)} fusion(f32[64,1792]{1,0:T(8,128)} %collective-permute-done.15, f32[2,64,1792]{2,1,0:T(8,128)S(1)} %proj.1), kind=kLoop, calls=%fused_computation.2 | loop fusion | flops 114688 | bytes 1376256 | tf_op jit(solution)/shard_map/add | solution.py:318
  (43 shorter events, 3.9 us)
Async XLA Ops:
  2.3 8.7 %collective-permute-start.1 = (bf16[128,576]{1,0:T(8,128)(2,1)}, bf16[128,576]{1,0:T(8,128)(2,1)S(1)}, u32[]{:S(2)}, u32[]{:S(2)}) collective-permute-start(bf16[128,576]{1,0:T(8,128)(2,1)} %pack.1.refs_2_), channel_id=1, source_target_pairs={{0,4},{4,8},{8,12},{12,16},{16,20},{20,24},{24,28},{28,0},{1,5},{5... | collective-permute-start | bytes 442376 | tf_op jit(solution)/shard_map/ppermute | solution.py:203
  2.8 9.9 %collective-permute-start = (bf16[128,576]{1,0:T(8,128)(2,1)}, bf16[128,576]{1,0:T(8,128)(2,1)S(1)}, u32[]{:S(2)}, u32[]{:S(2)}) collective-permute-start(bf16[128,576]{1,0:T(8,128)(2,1)} %pack.1.refs_2_), channel_id=1, source_target_pairs={{0,8},{4,12},{8,16},{12,20},{16,24},{20,28},{24,0},{28,4},{1,9},{5... | collective-permute-start | bytes 442376 | tf_op jit(solution)/shard_map/ppermute | solution.py:203
  5.4 27.7 %collective-permute-start.10 = (bf16[128,1792]{1,0:T(8,128)(2,1)}, bf16[128,1792]{1,0:T(8,128)(2,1)S(1)}, u32[]{:S(2)}, u32[]{:S(2)}) collective-permute-start(bf16[128,1792]{1,0:T(8,128)(2,1)} %refs_4_.1), channel_id=1, source_target_pairs={{0,8},{4,12},{8,0},{12,4},{16,24},{20,28},{24,16},{28,20},{1,9},{5... | collective-permute-start | bytes 1376264 | tf_op jit(solution)/shard_map/ppermute | solution.py:213
  12.7 0.9 %copy-start.3 = (bf16[128,576]{1,0:T(8,128)(2,1)S(1)}, bf16[128,576]{1,0:T(8,128)(2,1)}, u32[]{:S(2)}) copy-start(bf16[128,576]{1,0:T(8,128)(2,1)} %pack.1.refs_2_) | copy-start | bytes 442372
  13.7 0.7 copy-start.6
  20.8 1.0 %copy-start.7 = (bf16[4,272,512]{2,1,0:T(8,128)(2,1)}, bf16[4,272,512]{2,1,0:T(8,128)(2,1)S(1)}, u32[]{:S(2)}) copy-start(bf16[4,272,512]{2,1,0:T(8,128)(2,1)S(1)} %get-tuple-element.21.ds_ref) | copy-start | bytes 3342340
  21.8 10.6 %copy-start = (bf16[128,1792]{1,0:T(8,128)(2,1)S(1)}, bf16[128,1792]{1,0:T(8,128)(2,1)}, u32[]{:S(2)}) copy-start(bf16[128,1792]{1,0:T(8,128)(2,1)} %refs_4_.1) | copy-start | bytes 1376260
  28.3 8.2 %collective-permute-start.2 = (bf16[128,576]{1,0:T(8,128)(2,1)S(1)}, bf16[128,576]{1,0:T(8,128)(2,1)S(1)}, u32[]{:S(2)}, u32[]{:S(2)}) collective-permute-start(bf16[128,576]{1,0:T(8,128)(2,1)S(1)} %get-tuple-element.27), channel_id=1, source_target_pairs={{0,28},{4,0},{8,4},{12,8},{16,12},{20,16},{24,20},{28,24},{1,29},{... | collective-permute-start | bytes 442376 | tf_op jit(solution)/shard_map/ppermute | solution.py:292
  32.4 5.9 %collective-permute-start.3 = (bf16[128,576]{1,0:T(8,128)(2,1)S(1)}, bf16[128,576]{1,0:T(8,128)(2,1)S(1)}, u32[]{:S(2)}, u32[]{:S(2)}) collective-permute-start(bf16[128,576]{1,0:T(8,128)(2,1)S(1)} %get-tuple-element.28), channel_id=1, source_target_pairs={{0,24},{4,28},{8,0},{12,4},{16,8},{20,12},{24,16},{28,20},{1,25},{... | collective-permute-start | bytes 442376 | tf_op jit(solution)/shard_map/ppermute | solution.py:292
  32.4 10.1 %collective-permute-start.11 = (bf16[128,1792]{1,0:T(8,128)(2,1)S(1)}, bf16[128,1792]{1,0:T(8,128)(2,1)S(1)}, u32[]{:S(2)}, u32[]{:S(2)}) collective-permute-start(bf16[128,1792]{1,0:T(8,128)(2,1)S(1)} %copy-done), channel_id=1, source_target_pairs={{8,16},{12,20},{16,8},{20,12},{9,17},{13,21},{17,9},{21,13},{10,18... | collective-permute-start | bytes 1376264 | tf_op jit(solution)/shard_map/ppermute | solution.py:213
  33.1 10.7 %collective-permute-start.13 = (bf16[128,1792]{1,0:T(8,128)(2,1)S(1)}, bf16[128,1792]{1,0:T(8,128)(2,1)}, u32[]{:S(2)}, u32[]{:S(2)}) collective-permute-start(bf16[128,1792]{1,0:T(8,128)(2,1)S(1)} %collective-permute-done.10.refs_5_), channel_id=1, source_target_pairs={{8,16},{12,20},{16,8},{20,12},{9,17},{13,21},{17,9},{21,13},{10,18... | collective-permute-start | bytes 1376264 | tf_op jit(solution)/shard_map/ppermute | solution.py:213
  36.5 1.8 %copy-start.11 = (bf16[128,576]{1,0:T(8,128)(2,1)}, bf16[128,576]{1,0:T(8,128)(2,1)S(1)}, u32[]{:S(2)}) copy-start(bf16[128,576]{1,0:T(8,128)(2,1)S(1)} %collective-permute-done.2) | copy-start | bytes 442372
  38.3 0.7 copy-start.12
  39.0 7.8 %collective-permute-start.6 = (bf16[128,576]{1,0:T(8,128)(2,1)}, bf16[128,576]{1,0:T(8,128)(2,1)}, u32[]{:S(2)}, u32[]{:S(2)}) collective-permute-start(bf16[128,576]{1,0:T(8,128)(2,1)} %fusion.1), channel_id=1, source_target_pairs={{0,3},{1,2},{2,1},{3,0},{4,7},{5,6},{6,5},{7,4},{8,11},{9,10},{10,... | collective-permute-start | bytes 442376 | tf_op jit(solution)/shard_map/ppermute | solution.py:296
  41.8 6.9 %collective-permute-start.5 = (bf16[128,576]{1,0:T(8,128)(2,1)}, bf16[128,576]{1,0:T(8,128)(2,1)}, u32[]{:S(2)}, u32[]{:S(2)}) collective-permute-start(bf16[128,576]{1,0:T(8,128)(2,1)} %fusion.1), channel_id=1, source_target_pairs={{0,2},{1,3},{2,0},{3,1},{4,6},{5,7},{6,4},{7,5},{8,10},{9,11},{10,... | collective-permute-start | bytes 442376 | tf_op jit(solution)/shard_map/ppermute | solution.py:296
  42.3 6.6 %collective-permute-start.4 = (bf16[128,576]{1,0:T(8,128)(2,1)}, bf16[128,576]{1,0:T(8,128)(2,1)}, u32[]{:S(2)}, u32[]{:S(2)}) collective-permute-start(bf16[128,576]{1,0:T(8,128)(2,1)} %fusion.1), channel_id=1, source_target_pairs={{0,1},{1,0},{2,3},{3,2},{4,5},{5,4},{6,7},{7,6},{8,9},{9,8},{10,11... | collective-permute-start | bytes 442376 | tf_op jit(solution)/shard_map/ppermute | solution.py:296
  42.5 32.5 %copy-start.1 = (bf16[128,1792]{1,0:T(8,128)(2,1)}, bf16[128,1792]{1,0:T(8,128)(2,1)S(1)}, u32[]{:S(2)}) copy-start(bf16[128,1792]{1,0:T(8,128)(2,1)S(1)} %collective-permute-done.11.refs_6_) | copy-start | bytes 1376260
  42.5 32.5 %collective-permute-start.12 = (bf16[128,1792]{1,0:T(8,128)(2,1)S(1)}, bf16[128,1792]{1,0:T(8,128)(2,1)}, u32[]{:S(2)}, u32[]{:S(2)}) collective-permute-start(bf16[128,1792]{1,0:T(8,128)(2,1)S(1)} %collective-permute-done.11.refs_6_), channel_id=1, source_target_pairs={{8,0},{12,4},{16,24},{20,28},{9,1},{13,5},{17,25},{21,29},{10,2},{... | collective-permute-start | bytes 1376264 | tf_op jit(solution)/shard_map/ppermute | solution.py:213
  43.8 31.2 %collective-permute-start.14 = (bf16[128,1792]{1,0:T(8,128)(2,1)}, bf16[128,1792]{1,0:T(8,128)(2,1)}, u32[]{:S(2)}, u32[]{:S(2)}) collective-permute-start(bf16[128,1792]{1,0:T(8,128)(2,1)} %collective-permute-done.13.refs_8_), channel_id=1, source_target_pairs={{8,0},{12,4},{16,24},{20,28},{9,1},{13,5},{17,25},{21,29},{10,2},{... | collective-permute-start | bytes 1376264 | tf_op jit(solution)/shard_map/ppermute | solution.py:213
  50.3 17.4 %copy-start.9 = (bf16[128,576]{1,0:T(8,128)(2,1)}, bf16[128,576]{1,0:T(8,128)(2,1)S(1)}, u32[]{:S(2)}) copy-start(bf16[128,576]{1,0:T(8,128)(2,1)S(1)} %add_convert_fusion) | copy-start | bytes 442372
  50.5 23.9 %collective-permute-start.9 = (bf16[128,128]{1,0:T(8,128)(2,1)S(1)}, bf16[128,128]{1,0:T(8,128)(2,1)S(1)}, u32[]{:S(2)}, u32[]{:S(2)}) collective-permute-start(bf16[128,128]{1,0:T(8,128)(2,1)S(1)} %get-tuple-element.34), channel_id=1, source_target_pairs={{0,24},{4,28},{8,0},{12,4},{16,8},{20,12},{24,16},{28,20},{1,25},{... | collective-permute-start | bytes 98312 | tf_op jit(solution)/shard_map/ppermute | solution.py:306
  54.5 19.8 %collective-permute-start.8 = (bf16[128,128]{1,0:T(8,128)(2,1)S(1)}, bf16[128,128]{1,0:T(8,128)(2,1)S(1)}, u32[]{:S(2)}, u32[]{:S(2)}) collective-permute-start(bf16[128,128]{1,0:T(8,128)(2,1)S(1)} %get-tuple-element.35), channel_id=1, source_target_pairs={{0,16},{4,20},{8,24},{12,28},{16,0},{20,4},{24,8},{28,12},{1,17},{... | collective-permute-start | bytes 98312 | tf_op jit(solution)/shard_map/ppermute | solution.py:306
  65.8 8.6 %collective-permute-start.7 = (bf16[128,128]{1,0:T(8,128)(2,1)S(1)}, bf16[128,128]{1,0:T(8,128)(2,1)S(1)}, u32[]{:S(2)}, u32[]{:S(2)}) collective-permute-start(bf16[128,128]{1,0:T(8,128)(2,1)S(1)} %get-tuple-element.36), channel_id=1, source_target_pairs={{0,8},{4,12},{8,16},{12,20},{16,24},{20,28},{24,0},{28,4},{1,9},{5... | collective-permute-start | bytes 98312 | tf_op jit(solution)/shard_map/ppermute | solution.py:306
  74.3 0.6 copy-start.4
  75.0 1.0 %copy-start.2 = (bf16[128,1792]{1,0:T(8,128)(2,1)S(1)}, bf16[128,1792]{1,0:T(8,128)(2,1)}, u32[]{:S(2)}) copy-start(bf16[128,1792]{1,0:T(8,128)(2,1)} %copy-done.1) | copy-start | bytes 1376260
  76.0 0.8 copy-start.5
  76.8 2.5 %copy-start.8 = (bf16[4,272,512]{2,1,0:T(8,128)(2,1)S(1)}, bf16[4,272,512]{2,1,0:T(8,128)(2,1)}, u32[]{:S(2)}) copy-start(bf16[4,272,512]{2,1,0:T(8,128)(2,1)} %copy-done.7) | copy-start | bytes 3342340
  79.1 8.7 %collective-permute-start.15 = (f32[64,1792]{1,0:T(8,128)S(1)}, f32[64,1792]{1,0:T(8,128)}, u32[]{:S(2)}, u32[]{:S(2)}) collective-permute-start(f32[64,1792]{1,0:T(8,128)S(1)} %slice_bitcast_fusion), channel_id=1, source_target_pairs={{0,4},{4,0},{8,12},{12,8},{16,20},{20,16},{24,28},{28,24},{1,5},{5... | collective-permute-start | bytes 1376264 | tf_op jit(solution)/shard_map/ppermute | solution.py:318
  79.2 7.3 %copy-start.10 = (bf16[128,576]{1,0:T(8,128)(2,1)S(1)}, bf16[128,576]{1,0:T(8,128)(2,1)}, u32[]{:S(2)}) copy-start(bf16[128,576]{1,0:T(8,128)(2,1)} %copy-done.9) | copy-start | bytes 442372
  79.2 7.9 %slice-start = ((bf16[128,576]{1,0:T(8,128)(2,1)}), bf16[128,64]{1,0:T(8,128)(2,1)S(1)}, s32[]{:S(2)}) async-start(bf16[128,576]{1,0:T(8,128)(2,1)} %copy-done.9), calls=%async_computation | async-start | bytes 65536 | tf_op jit(solution)/shard_map/slice | solution.py:299

commit v2 on v1

v2 whole, which is shorter than its diff:
```python
import functools

import jax
import jax.numpy as jnp
from jax import lax
from jax.experimental import pallas as pl
from jax.experimental.pallas import tpu as pltpu
from jax.sharding import PartitionSpec as P


WIN_BLK = 3
DOCS = 4
CHUNK = 16
PAIR = 2
LANES = 128
DOC_VALUES = 8

softmax_scale = 192.0 ** (-0.5)


def nt(a, b):
    return lax.dot_general(a, b, (((1,), (1,)), ((), ())), preferred_element_type=jnp.float32)


def nn(a, b):
    return lax.dot_general(a, b, (((1,), (0,)), ((), ())), preferred_element_type=jnp.float32)


def tn(a, b):
    return lax.dot_general(a, b, (((0,), (0,)), ((), ())), preferred_element_type=jnp.float32)


def score_step(begin, keys_ref, first_ref, q_ref, qr_ref, do_ref, ds_ref, acc_ref, turn_ref, *, width, lat, heads, window):
    keys = keys_ref[pl.ds(begin, width), :]
    klat = keys[:, :lat]
    q = q_ref[...]
    do = do_ref[...]
    block = q.shape[0]
    rope = turn_ref.shape[1]
    turned = qr_ref[...].astype(jnp.float32)
    for head in range(heads):
        turn_ref[pl.ds(head, CHUNK, stride=heads), :] = turned[:, head * rope:(head + 1) * rope]
    qr = turn_ref[...].astype(jnp.bfloat16)
    firsts = []
    lasts = []
    for at in range(0, block, LANES):
        token = begin + (lax.broadcasted_iota(jnp.int32, first_ref.shape, 1) + at) // heads
        firsts.append(jnp.take_along_axis(first_ref[...], token, axis=1, mode="promise_in_bounds")[:1])
        lasts.append(token[:1] + window)
    first = jnp.concatenate(firsts, axis=1)
    last = jnp.concatenate(lasts, axis=1)
    scores = nt(klat, q) + nt(keys[:, lat:], qr)
    pos = lax.broadcasted_iota(jnp.int32, scores.shape, 0) + begin
    allowed = (pos >= first) & (pos <= last)
    scores = jnp.where(allowed, scores, -jnp.inf)
    top = jnp.max(scores, axis=0, keepdims=True)
    expo = jnp.exp((scores - top) * softmax_scale)
    inverse = 1.0 / jnp.sum(expo, axis=0, keepdims=True)
    probs = expo * inverse
    low = probs.astype(jnp.bfloat16)
    dprob = nt(klat, do)
    delta = jnp.sum(low.astype(jnp.float32) * dprob, axis=0, keepdims=True)
    ds = (probs * (dprob - delta) * softmax_scale).astype(jnp.bfloat16)
    ds_ref[0] = ds
    acc_ref[pl.ds(begin, width), :lat] += nn(ds, q) + nn(low, do)
    acc_ref[pl.ds(begin, width), lat:] += nn(ds, qr)


def score_kernel(place_ref, doc_ref, q_ref, qr_ref, do_ref, *refs, width, lat, heads, window, slots):
    blocks, ropes, refs = refs[:slots], refs[slots:2 * slots], refs[2 * slots:]
    (ds_ref, keys_ref), part_refs, (acc_ref, first_ref, turn_ref) = refs[:2], refs[2:-3], refs[-3:]
    tok = blocks[0].shape[0]
    step = pl.program_id(0)

    @pl.when(step == 0)
    def _():
        acc_ref[...] = jnp.zeros_like(acc_ref)
        for slot in range(slots):
            rows = slice(slot * tok, (slot + 1) * tok)
            keys_ref[rows, :lat] = blocks[slot][...]
            keys_ref[rows, lat:] = ropes[slot][...].astype(jnp.float32).T.astype(keys_ref.dtype)
        rank = place_ref[0]
        ids = doc_ref[...]
        mine = doc_ref[pl.ds(rank, 1), :]
        begins = jnp.zeros(mine.shape, jnp.float32)
        for value in range(DOC_VALUES - 1):
            count = jnp.sum(jnp.where(ids == value, 1.0, 0.0), axis=0, keepdims=True)
            count = jnp.sum(count, axis=1, keepdims=True)
            begins += jnp.where(mine > value, count, 0.0)
        here = lax.broadcasted_iota(jnp.int32, mine.shape, 1) + rank * tok
        first = jnp.maximum(begins.astype(jnp.int32), here - (window - 1)) - (rank * tok - window)
        first_ref[...] = jnp.broadcast_to(first, first_ref.shape)

    begin = pl.multiple_of(step * CHUNK, CHUNK)
    score_step(begin, keys_ref, first_ref, q_ref, qr_ref, do_ref, ds_ref, acc_ref, turn_ref,
               width=width, lat=lat, heads=heads, window=window)

    @pl.when(step == pl.num_programs(0) - 1)
    def _():
        for slot, part_ref in enumerate(part_refs):
            part_ref[...] = acc_ref[slot * tok:(slot + 1) * tok, :].astype(part_ref.dtype)


def query_kernel(ds_ref, keys_ref, *refs, width, lat, heads, offset):
    dq_ref, dqr_ref, turn_ref = refs[-3:]
    begin = pl.multiple_of((pl.program_id(0) + offset) * CHUNK, CHUNK)
    keys = keys_ref[pl.ds(begin, width), :]
    ds = ds_ref[0]
    dq_ref[...] = tn(ds, keys[:, :lat]).astype(dq_ref.dtype)
    turn_ref[...] = tn(ds, keys[:, lat:])
    rope = turn_ref.shape[1]
    for head in range(0, heads, 2):
        pair = [turn_ref[pl.ds(head + which, CHUNK, stride=heads), :] for which in range(2)]
        dqr_ref[:, head * rope:(head + 2) * rope] = jnp.concatenate(pair, axis=1).astype(dqr_ref.dtype)


def proj_kernel(place_ref, own_ref, mail_ref, here_ref, near_ref, keep_ref, give_ref):
    count, half, span = keep_ref.shape
    north = place_ref[0] == 1
    own = own_ref[...]
    mail = mail_ref[...]
    for at in range(0, span, 2 * LANES):
        lanes = slice(at, min(at + 2 * LANES, span))
        product = tn(own, here_ref[:, lanes]) + tn(mail, near_ref[:, lanes])
        for group in range(count):
            low = product[PAIR * group * half:(PAIR * group + 1) * half]
            high = product[(PAIR * group + 1) * half:(PAIR * group + 2) * half]
            keep_ref[place_ref[1] ^ group, :, lanes] = jnp.where(north, high, low)
            give_ref[place_ref[1] ^ group, :, lanes] = jnp.where(north, low, high).astype(give_ref.dtype)


def ring(peers, by):
    return [(i, (i + by) % peers) for i in range(peers)]


def across(peers, by):
    return [(i, i ^ by) for i in range(peers)]


def in_hbm(array):
    return pltpu.with_memory_space_constraint(array, pltpu.HBM)


def shards(q_latent, q_rope, latent, key_rope, out_grad, inputs, doc_ids):
    tok, heads, lat = q_latent.shape
    rope = key_rope.shape[1]
    total = doc_ids.shape[0]
    ctxs = lax.axis_size("ctx")
    headers = lax.axis_size("head")
    window = min(WIN_BLK * tok, total // DOCS)
    depth = window // tok
    slots = depth + 1
    rank = lax.axis_index("ctx")
    rows = tok * heads
    steps = tok // CHUNK
    block = CHUNK * heads
    keyed = lat + rope
    groups = ctxs // PAIR
    low = jnp.bfloat16
    smem = pl.BlockSpec(memory_space=pltpu.SMEM)
    whole_of = pl.BlockSpec(memory_space=pltpu.VMEM)

    blocks = [lax.ppermute(latent, "ctx", ring(ctxs, back)) for back in range(depth, 0, -1)] + [latent]
    turned = key_rope.T
    ropes = [lax.ppermute(turned, "ctx", ring(ctxs, back)) for back in range(depth, 0, -1)] + [turned]
    near = lax.ppermute(inputs, "ctx", across(ctxs, PAIR))

    q = q_latent.reshape(rows, lat)
    do = out_grad.reshape(rows, lat)
    span = window + tok
    width = window + CHUNK
    places = rank.astype(jnp.int32).reshape(1)
    split = steps // 2
    resident = lambda *shape: pl.BlockSpec(shape, lambda i: (0,) * len(shape))
    limits = pltpu.CompilerParams(dimension_semantics=("arbitrary",), vmem_limit_bytes=20 * 1024 * 1024)
    sizes = dict(width=width, lat=lat, heads=heads, window=window)

    def tiles(offset):
        return [
            pl.BlockSpec((block, lat), lambda i: (i + offset, 0)),
            pl.BlockSpec((CHUNK, heads * rope), lambda i: (i + offset, 0)),
            pl.BlockSpec((block, lat), lambda i: (i + offset, 0)),
        ]

    turner = pltpu.VMEM((block, rope), jnp.float32)
    ds, keys, *part = pl.pallas_call(
        functools.partial(score_kernel, slots=slots, **sizes),
        grid=(steps,),
        in_specs=[smem, resident(ctxs, tok)] + tiles(0) + [resident(tok, lat)] * slots + [resident(rope, tok)] * slots,
        out_specs=[pl.BlockSpec((1, width, block), lambda i: (i, 0, 0)), resident(span, keyed)] + [resident(tok, keyed)] * slots,
        out_shape=[jax.ShapeDtypeStruct((steps, width, block), low), jax.ShapeDtypeStruct((span, keyed), low)]
        + [jax.ShapeDtypeStruct((tok, keyed), low)] * slots,
        scratch_shapes=[pltpu.VMEM((span, keyed), jnp.float32), pltpu.VMEM((8, tok), jnp.int32), turner],
        compiler_params=limits,
        name="score",
    )(places, in_hbm(doc_ids.reshape(ctxs, tok)), in_hbm(q), in_hbm(q_rope), in_hbm(do), *blocks[:-1], in_hbm(latent), *ropes[:-1], in_hbm(turned))

    shapes = [jax.ShapeDtypeStruct((rows, lat), low), jax.ShapeDtypeStruct((tok, heads * rope), low)]
    grads = ()
    for call in range(2):
        offset = call * split
        grads = pl.pallas_call(
            functools.partial(query_kernel, width=width, lat=lat, heads=heads, offset=offset),
            grid=(split,),
            in_specs=[pl.BlockSpec((1, width, block), lambda i, offset=offset: (i + offset, 0, 0)), resident(span, keyed)] + [pl.BlockSpec(memory_space=pl.ANY)] * len(grads),
            out_specs=tiles(offset)[:2],
            out_shape=shapes,
            scratch_shapes=[turner],
            input_output_aliases={2: 0, 3: 1} if call else {},
            compiler_params=pltpu.CompilerParams(dimension_semantics=("arbitrary",), vmem_limit_bytes=10 * 1024 * 1024),
            name="query",
        )(ds, keys, *[in_hbm(grad) for grad in grads])
    q_latent_grad = grads[0].reshape(tok, heads, lat)
    q_rope_grad = grads[1]

    mine = part[depth].astype(jnp.float32)
    for back in range(1, depth + 1):
        mine = mine + lax.ppermute(part[depth - back], "ctx", ring(ctxs, -back)).astype(jnp.float32)
    sent = lax.optimization_barrier(mine.astype(low))
    terms = [sent.astype(jnp.float32)]
    for by in range(1, headers):
        terms.append(lax.ppermute(sent, "head", across(headers, by)).astype(jnp.float32))
    while len(terms) > 1:
        terms = [left + right for left, right in zip(terms[::2], terms[1::2])]
    found = terms[0].astype(low)
    latent_grad = found[:, :lat]
    key_rope_grad = found[:, lat:]

    narrow = PAIR * lat // ctxs
    count = groups // 2
    odd = (rank // PAIR) % 2

    def columns(parity):
        taken = [lax.dynamic_slice_in_dim(found, (2 * group + parity) * narrow, narrow, 1) for group in range(count)]
        return jnp.concatenate(taken, axis=1)

    mail = lax.ppermute(columns(1 - odd), "ctx", across(ctxs, PAIR))
    words = jnp.stack([rank % PAIR, rank // (2 * PAIR)]).astype(jnp.int32)
    half, width_in = lat // ctxs, inputs.shape[1]
    keep, give = pl.pallas_call(
        proj_kernel,
        in_specs=[smem] + [whole_of] * 4,
        out_specs=[whole_of] * 2,
        out_shape=[jax.ShapeDtypeStruct((count, half, width_in), jnp.float32), jax.ShapeDtypeStruct((count, half, width_in), low)],
        compiler_params=pltpu.CompilerParams(vmem_limit_bytes=24 * 1024 * 1024),
        name="proj",
    )(words, columns(odd), mail, inputs, near)
    keep = keep + lax.ppermute(give, "ctx", across(ctxs, 1)).astype(jnp.float32)
    while count > 1:
        count //= 2
        keep = keep[:count] + lax.ppermute(keep[count:].astype(low), "ctx", across(ctxs, 2 * PAIR * count)).astype(jnp.float32)
    proj_grad = keep[0]
    return (q_latent_grad, q_rope_grad, latent_grad, key_rope_grad, proj_grad)


def solution(mesh):
    placed = (
        P("ctx", "head", None),
        P("ctx", "head"),
        P("ctx", None),
        P("ctx", None),
        P("ctx", "head", None),
        P("ctx", "head"),
        P(),
    )

    return jax.shard_map(
        shards,
        mesh=mesh,
        in_specs=placed,
        out_specs=(
            P("ctx", "head", None),
            P("ctx", "head"),
            P("ctx", None),
            P("ctx", None),
            P("ctx", "head"),
        ),
        check_vma=False,
    )
```

time: 90.2 us -> 66.8 us (0.74)
  starting transfers between devices: 34.2 us -> 14.2 us
  waiting for transfers between devices: 19.8 us -> 26.1 us
  local copies, waits for them, and re-layouts: 6.62 us -> 1.54 us
  Pallas kernels: 24.2 us -> 20.8 us
    ppermute x11 -> x8, starting transfers between devices: 26.7 us -> 8.86 us  [the longest x2 3.11 us: shards(): lax.ppermute(latent, 'ctx', ring(ctxs, back))]
    unnamed x27 -> x5, local copies, waits for them, and re-layouts: 5.7 us -> 0.71 us
    ppermute x3, waiting for transfers between devices: 3.84 us -> 7.42 us  [shards(): lax.ppermute(sent, 'head', across(headers, by)).astype(jnp.float32)]
    pallas_call x4 -> x2, Pallas kernels: 17 us -> 13.6 us  [the longest x1 11.9 us: shards(): pl.pallas_call(functools.partial(score_kernel, slots=slots, **sizes), gri...]
    ppermute x2, starting transfers between devices: 4.06 us -> 1.79 us  [shards(): lax.ppermute(part[depth - back], 'ctx', ring(ctxs, -back))]
    squeeze x0 -> x1, other arithmetic: none -> 1.82 us  [shards(): proj_grad = keep[0]]
    add x1, other arithmetic: 1.83 us -> 0.1 us  [shards(): keep = keep + lax.ppermute(give, 'ctx', across(ctxs, 1)).astype(jnp.float32)]
    ppermute x2, waiting for transfers between devices: 3.73 us -> 5.14 us  [shards(): lax.ppermute(part[depth - back], 'ctx', ring(ctxs, -back))]
  transfers between devices with their start and end apart: 16 -> 13, of which waited for: 8 -> 11; matrix products, arithmetic and copies ran while one was open for 4% -> 4% of each run, Pallas kernels for 23% -> 11%
where the time goes in v2:
time: 66.8 us; the launch traced here: 66.5 us
  waiting for transfers between devices  26.1 us (39%)
  Pallas kernels  20.8 us (31%)
  starting transfers between devices  14.2 us (21%)
  other arithmetic  3.16 us (5%)
  local copies, waits for them, and re-layouts  1.54 us (2%)
  between operations  0.73 us (1%)
    pallas_call x1, Pallas kernels, shards(): pl.pallas_call(functools.partial(score_kernel, slots=slots, **sizes), gri...  11.9 us
    ppermute x3, waiting for transfers between devices, shards(): lax.ppermute(sent, 'head', across(headers, by)).astype(jnp.float32)  7.42 us
    pallas_call x2, Pallas kernels, shards(): pl.pallas_call(functools.partial(query_kernel, width=width, lat=lat, head...  7.23 us
    ppermute x2, waiting for transfers between devices, shards(): lax.ppermute(part[depth - back], 'ctx', ring(ctxs, -back))  5.14 us
    ppermute x2, waiting for transfers between devices, shards(): lax.ppermute(turned, 'ctx', ring(ctxs, back))  4.67 us
    ppermute x1, waiting for transfers between devices, shards(): near = lax.ppermute(inputs, 'ctx', across(ctxs, PAIR))  3.63 us
    ppermute x3, starting transfers between devices, shards(): lax.ppermute(sent, 'head', across(headers, by)).astype(jnp.float32)  3.55 us
    ppermute x2, starting transfers between devices, shards(): lax.ppermute(latent, 'ctx', ring(ctxs, back))  3.11 us
  transfers between devices with their start and end apart: 13, of which 11 were waited for; matrix products, arithmetic and copies ran while one was open for 4% of the time, Pallas kernels for 11%

profile of v2, /device:TPU:0, one launch (start us, length us, event | category | flops | bytes accessed | tf_op | source)
XLA Modules:
  0.0 66.5 jit_solution(10691400240371232413)
XLA Ops:
  0.6 3.1 %collective-permute-start = (bf16[128,512]{1,0:T(8,128)(2,1)}, bf16[128,512]{1,0:T(8,128)(2,1)S(1)}, u32[]{:S(2)}, u32[]{:S(2)}) collective-permute-start(bf16[128,512]{1,0:T(8,128)(2,1)} %refs_2_.1), channel_id=1, source_target_pairs={{0,8},{4,12},{8,16},{12,20},{16,24},{20,28},{24,0},{28,4},{1,9},{5... | collective-permute-start | bytes 393224 | tf_op jit(solution)/shard_map/ppermute | solution.py:163
  3.7 1.6 %collective-permute-start.2 = (bf16[64,128]{1,0:T(8,128)(2,1)}, bf16[64,128]{1,0:T(8,128)(2,1)S(1)}, u32[]{:S(2)}, u32[]{:S(2)}) collective-permute-start(bf16[64,128]{1,0:T(8,128)(2,1)} %bitcast.13), channel_id=1, source_target_pairs={{0,8},{4,12},{8,16},{12,20},{16,24},{20,28},{24,0},{28,4},{1,9},{5... | collective-permute-start | bytes 49160 | tf_op jit(solution)/shard_map/ppermute | solution.py:165
  5.3 1.4 %collective-permute-start.3 = (bf16[64,128]{1,0:T(8,128)(2,1)}, bf16[64,128]{1,0:T(8,128)(2,1)S(1)}, u32[]{:S(2)}, u32[]{:S(2)}) collective-permute-start(bf16[64,128]{1,0:T(8,128)(2,1)} %bitcast.14), channel_id=1, source_target_pairs={{0,4},{4,8},{8,12},{12,16},{16,20},{20,24},{24,28},{28,0},{1,5},{5... | collective-permute-start | bytes 49160 | tf_op jit(solution)/shard_map/ppermute | solution.py:165
  6.7 3.8 %collective-permute-done.2.refs_3_ = bf16[64,128]{1,0:T(8,128)(2,1)S(1)} collective-permute-done((bf16[64,128]{1,0:T(8,128)(2,1)}, bf16[64,128]{1,0:T(8,128)(2,1)S(1)}, u32[]{:S(2)}, u32[]{:S(2)}) %collective-permute-start.2) | collective-permute-done | bytes 16416 | tf_op jit(solution)/shard_map/ppermute | solution.py:165
  10.6 0.8 %collective-permute-done.3.refs_4_ = bf16[64,128]{1,0:T(8,128)(2,1)S(1)} collective-permute-done((bf16[64,128]{1,0:T(8,128)(2,1)}, bf16[64,128]{1,0:T(8,128)(2,1)S(1)}, u32[]{:S(2)}, u32[]{:S(2)}) %collective-permute-start.3) | collective-permute-done | bytes 16416 | tf_op jit(solution)/shard_map/ppermute | solution.py:165
  11.4 11.9 %score.1 = (bf16[8,272,512]{2,1,0:T(8,128)(2,1)S(1)}, bf16[384,576]{1,0:T(8,128)(2,1)S(1)}, bf16[128,576]{1,0:T(8,128)(2,1)S(1)}, bf16[128,576]{1,0:T(8,128)(2,1)S(1)}, bf16[128,576]{1,0:T(8,128)(2,1)S(1)}) custom-call(s32[1]{0:T(128)} %bitcast.place_ref, s32[8,128]{1,0:T(8,128)} %bitcast.16, bf16[4096,512]{1,0:T(8,128)(2,1)} %bitcast.11, ...), custom_call_target="tpu_custom_call" | custom-call | tf_op jit(solution)/shard_map/score/pallas_call | solution.py:186
  23.3 1.8 %collective-permute-start.5 = (bf16[128,576]{1,0:T(8,128)(2,1)S(1)}, bf16[128,576]{1,0:T(8,128)(2,1)S(1)}, u32[]{:S(2)}, u32[]{:S(2)}) collective-permute-start(bf16[128,576]{1,0:T(8,128)(2,1)S(1)} %get-tuple-element.24), channel_id=1, source_target_pairs={{0,24},{4,28},{8,0},{12,4},{16,8},{20,12},{24,16},{28,20},{1,25},{... | collective-permute-start | bytes 442376 | tf_op jit(solution)/shard_map/ppermute | solution.py:218
  25.1 4.1 %collective-permute-done.5 = bf16[128,576]{1,0:T(8,128)(2,1)S(1)} collective-permute-done((bf16[128,576]{1,0:T(8,128)(2,1)S(1)}, bf16[128,576]{1,0:T(8,128)(2,1)S(1)}, u32[]{:S(2)}, u32[]{:S(2)}) %collective-permute-start.5) | collective-permute-done | bytes 147488 | tf_op jit(solution)/shard_map/ppermute | solution.py:218
  29.2 1.0 %collective-permute-done.4 = bf16[128,576]{1,0:T(8,128)(2,1)S(1)} collective-permute-done((bf16[128,576]{1,0:T(8,128)(2,1)S(1)}, bf16[128,576]{1,0:T(8,128)(2,1)S(1)}, u32[]{:S(2)}, u32[]{:S(2)}) %collective-permute-start.4) | collective-permute-done | bytes 147488 | tf_op jit(solution)/shard_map/ppermute | solution.py:218
  30.3 2.5 %collective-permute-start.8 = (bf16[128,576]{1,0:T(8,128)(2,1)S(1)}, bf16[128,576]{1,0:T(8,128)(2,1)S(1)}, u32[]{:S(2)}, u32[]{:S(2)}) collective-permute-start(bf16[128,576]{1,0:T(8,128)(2,1)S(1)} %add_convert_fusion.1), channel_id=1, source_target_pairs={{0,3},{1,2},{2,1},{3,0},{4,7},{5,6},{6,5},{7,4},{8,11},{9,10},{10,... | collective-permute-start | bytes 442376 | tf_op jit(solution)/shard_map/ppermute | solution.py:222
  32.8 0.5 collective-permute-start.7
  33.3 0.5 collective-permute-start.6
  33.9 0.3 collective-permute-start.10
  34.1 0.1 pad_add_fusion.place_ref
  34.2 4.1 %collective-permute-done.8 = bf16[128,576]{1,0:T(8,128)(2,1)S(1)} collective-permute-done((bf16[128,576]{1,0:T(8,128)(2,1)S(1)}, bf16[128,576]{1,0:T(8,128)(2,1)S(1)}, u32[]{:S(2)}, u32[]{:S(2)}) %collective-permute-start.8) | collective-permute-done | bytes 147488 | tf_op jit(solution)/shard_map/ppermute | solution.py:222
  38.4 3.2 %collective-permute-done.7 = bf16[128,576]{1,0:T(8,128)(2,1)} collective-permute-done((bf16[128,576]{1,0:T(8,128)(2,1)S(1)}, bf16[128,576]{1,0:T(8,128)(2,1)}, u32[]{:S(2)}, u32[]{:S(2)}) %collective-permute-start.7) | collective-permute-done | bytes 147488 | tf_op jit(solution)/shard_map/ppermute | solution.py:222
  41.6 0.1 collective-permute-done.6
  41.6 1.1 %add_convert_fusion = bf16[128,576]{1,0:T(8,128)(2,1)S(1)} fusion(bf16[128,576]{1,0:T(8,128)(2,1)S(1)} %collective-permute-done.8, bf16[128,576]{1,0:T(8,128)(2,1)} %collective-permute-done.7, bf16[128,576]{1,0:T(8,128)(2,1)} %collective-permute-done.6, bf16[128,576]{1,0:T(8,128)(2,1)S(1)} %add_convert_fusion.1), kind=kLoop, calls=%fused_computation.4 | loop fusion | flops 589824 | bytes 737280 | tf_op jit(solution)/shard_map/convert_element_type | solution.py:225
  42.7 0.1 constant_dynamic-slice_fusion.1
  42.9 0.1 collective-permute-start.9
  43.0 3.6 %collective-permute-done.10.near_ref = bf16[128,1792]{1,0:T(8,128)(2,1)} collective-permute-done((bf16[128,1792]{1,0:T(8,128)(2,1)S(1)}, bf16[128,1792]{1,0:T(8,128)(2,1)}, u32[]{:S(2)}, u32[]{:S(2)}) %collective-permute-start.10) | collective-permute-done | bytes 458784 | tf_op jit(solution)/shard_map/ppermute | solution.py:166
  46.6 0.8 %collective-permute-done.9.mail_ref = bf16[128,256]{1,0:T(8,128)(2,1)S(1)} collective-permute-done((bf16[128,256]{1,0:T(8,128)(2,1)S(1)}, bf16[128,256]{1,0:T(8,128)(2,1)S(1)}, u32[]{:S(2)}, u32[]{:S(2)}) %collective-permute-start.9) | collective-permute-done | bytes 65568 | tf_op jit(solution)/shard_map/ppermute | solution.py:237
  47.4 1.7 %proj.1 = (f32[2,64,1792]{2,1,0:T(8,128)S(1)}, bf16[2,64,1792]{2,1,0:T(8,128)(2,1)S(1)}) custom-call(s32[2]{0:T(128)S(1)} %pad_add_fusion.place_ref, bf16[128,256]{1,0:T(8,128)(2,1)S(1)} %pad_maximum_fusion.own_ref, bf16[128,256]{1,0:T(8,128)(2,1)S(1)} %collective-permute-done.9.mail_ref, bf16[128,1792]{1,0:T(8,128)(2,1)S(1)} %copy-done, ...), custom_call_target="tpu_custom_call" | custom-call | tf_op jit(solution)/shard_map/proj/pallas_call | solution.py:240
  49.2 1.8 %collective-permute-done.11 = bf16[2,64,1792]{2,1,0:T(8,128)(2,1)S(1)} collective-permute-done((bf16[2,64,1792]{2,1,0:T(8,128)(2,1)S(1)}, bf16[2,64,1792]{2,1,0:T(8,128)(2,1)S(1)}, u32[]{:S(2)}, u32[]{:S(2)}) %collective-permute-start.11) | collective-permute-done | bytes 458784 | tf_op jit(solution)/shard_map/ppermute | solution.py:248
  51.0 0.1 convert_add_fusion
  51.2 2.3 %collective-permute-start.12 = (bf16[1,64,1792]{2,1,0:T(8,128)(2,1)S(1)}, bf16[1,64,1792]{2,1,0:T(8,128)(2,1)S(1)}, u32[]{:S(2)}, u32[]{:S(2)}) collective-permute-start(bf16[1,64,1792]{2,1,0:T(8,128)(2,1)S(1)} %slice.25), channel_id=1, source_target_pairs={{0,16},{4,20},{8,24},{12,28},{16,0},{20,4},{24,8},{28,12},{1,17},{... | collective-permute-start | bytes 688136 | tf_op jit(solution)/shard_map/ppermute | solution.py:251
  53.5 3.6 %query.2 = (bf16[4096,512]{1,0:T(8,128)(2,1)}, bf16[128,2048]{1,0:T(8,128)(2,1)}) custom-call(bf16[8,272,512]{2,1,0:T(8,128)(2,1)S(1)} %get-tuple-element.16.ds_ref, bf16[384,576]{1,0:T(8,128)(2,1)S(1)} %get-tuple-element.17.keys_ref), custom_call_target="tpu_custom_call" | custom-call | tf_op jit(solution)/shard_map/query/pallas_call | solution.py:202
  57.1 3.6 %query.3 = (bf16[4096,512]{1,0:T(8,128)(2,1)}, bf16[128,2048]{1,0:T(8,128)(2,1)}) custom-call(bf16[8,272,512]{2,1,0:T(8,128)(2,1)S(1)} %get-tuple-element.16.ds_ref, bf16[384,576]{1,0:T(8,128)(2,1)S(1)} %get-tuple-element.17.keys_ref, bf16[4096,512]{1,0:T(8,128)(2,1)} %get-tuple-element.18.refs_0_, ...), custom_call_target="tpu_custom_call", output_to_operand_aliasing={{0}: (2, {}), {1}: (3, {})} | custom-call | tf_op jit(solution)/shard_map/query/pallas_call | solution.py:202
  60.7 0.7 slice.17
  61.4 0.7 %copy.14 = bf16[128,64]{0,1:T(8,128)(2,1)} copy(bf16[128,64]{1,0:T(8,128)(2,1)S(1)} %slice.18) | data formatting | bytes 32768
  62.1 2.6 %collective-permute-done.12 = bf16[1,64,1792]{2,1,0:T(8,128)(2,1)S(1)} collective-permute-done((bf16[1,64,1792]{2,1,0:T(8,128)(2,1)S(1)}, bf16[1,64,1792]{2,1,0:T(8,128)(2,1)S(1)}, u32[]{:S(2)}, u32[]{:S(2)}) %collective-permute-start.12) | collective-permute-done | bytes 229408 | tf_op jit(solution)/shard_map/ppermute | solution.py:251
  64.7 1.8 %fusion = f32[64,1792]{1,0:T(8,128)} fusion(f32[2,64,1792]{2,1,0:T(8,128)} %copy-done.1, bf16[1,64,1792]{2,1,0:T(8,128)(2,1)S(1)} %collective-permute-done.12), kind=kLoop, calls=%fused_computation.3 | loop fusion | flops 229376 | bytes 1146880 | tf_op jit(solution)/shard_map/squeeze | solution.py:252
  (14 shorter events, 0.2 us)
Async XLA Ops:
  0.6 10.8 %collective-permute-start = (bf16[128,512]{1,0:T(8,128)(2,1)}, bf16[128,512]{1,0:T(8,128)(2,1)S(1)}, u32[]{:S(2)}, u32[]{:S(2)}) collective-permute-start(bf16[128,512]{1,0:T(8,128)(2,1)} %refs_2_.1), channel_id=1, source_target_pairs={{0,8},{4,12},{8,16},{12,20},{16,24},{20,28},{24,0},{28,4},{1,9},{5... | collective-permute-start | bytes 393224 | tf_op jit(solution)/shard_map/ppermute | solution.py:163
  3.7 7.7 %collective-permute-start.1 = (bf16[128,512]{1,0:T(8,128)(2,1)}, bf16[128,512]{1,0:T(8,128)(2,1)S(1)}, u32[]{:S(2)}, u32[]{:S(2)}) collective-permute-start(bf16[128,512]{1,0:T(8,128)(2,1)} %refs_2_.1), channel_id=1, source_target_pairs={{0,4},{4,8},{8,12},{12,16},{16,20},{20,24},{24,28},{28,0},{1,5},{5... | collective-permute-start | bytes 393224 | tf_op jit(solution)/shard_map/ppermute | solution.py:163
  3.7 6.8 %collective-permute-start.2 = (bf16[64,128]{1,0:T(8,128)(2,1)}, bf16[64,128]{1,0:T(8,128)(2,1)S(1)}, u32[]{:S(2)}, u32[]{:S(2)}) collective-permute-start(bf16[64,128]{1,0:T(8,128)(2,1)} %bitcast.13), channel_id=1, source_target_pairs={{0,8},{4,12},{8,16},{12,20},{16,24},{20,28},{24,0},{28,4},{1,9},{5... | collective-permute-start | bytes 49160 | tf_op jit(solution)/shard_map/ppermute | solution.py:165
  5.3 6.1 %collective-permute-start.3 = (bf16[64,128]{1,0:T(8,128)(2,1)}, bf16[64,128]{1,0:T(8,128)(2,1)S(1)}, u32[]{:S(2)}, u32[]{:S(2)}) collective-permute-start(bf16[64,128]{1,0:T(8,128)(2,1)} %bitcast.14), channel_id=1, source_target_pairs={{0,4},{4,8},{8,12},{12,16},{16,20},{20,24},{24,28},{28,0},{1,5},{5... | collective-permute-start | bytes 49160 | tf_op jit(solution)/shard_map/ppermute | solution.py:165
  11.4 22.4 %copy-start = (bf16[128,1792]{1,0:T(8,128)(2,1)S(1)}, bf16[128,1792]{1,0:T(8,128)(2,1)}, u32[]{:S(2)}) copy-start(bf16[128,1792]{1,0:T(8,128)(2,1)} %here_ref.1) | copy-start | bytes 1376260
  23.3 5.9 %collective-permute-start.5 = (bf16[128,576]{1,0:T(8,128)(2,1)S(1)}, bf16[128,576]{1,0:T(8,128)(2,1)S(1)}, u32[]{:S(2)}, u32[]{:S(2)}) collective-permute-start(bf16[128,576]{1,0:T(8,128)(2,1)S(1)} %get-tuple-element.24), channel_id=1, source_target_pairs={{0,24},{4,28},{8,0},{12,4},{16,8},{20,12},{24,16},{28,20},{1,25},{... | collective-permute-start | bytes 442376 | tf_op jit(solution)/shard_map/ppermute | solution.py:218
  25.1 5.1 %collective-permute-start.4 = (bf16[128,576]{1,0:T(8,128)(2,1)S(1)}, bf16[128,576]{1,0:T(8,128)(2,1)S(1)}, u32[]{:S(2)}, u32[]{:S(2)}) collective-permute-start(bf16[128,576]{1,0:T(8,128)(2,1)S(1)} %get-tuple-element.23), channel_id=1, source_target_pairs={{0,28},{4,0},{8,4},{12,8},{16,12},{20,16},{24,20},{28,24},{1,29},{... | collective-permute-start | bytes 442376 | tf_op jit(solution)/shard_map/ppermute | solution.py:218
  30.3 8.1 %collective-permute-start.8 = (bf16[128,576]{1,0:T(8,128)(2,1)S(1)}, bf16[128,576]{1,0:T(8,128)(2,1)S(1)}, u32[]{:S(2)}, u32[]{:S(2)}) collective-permute-start(bf16[128,576]{1,0:T(8,128)(2,1)S(1)} %add_convert_fusion.1), channel_id=1, source_target_pairs={{0,3},{1,2},{2,1},{3,0},{4,7},{5,6},{6,5},{7,4},{8,11},{9,10},{10,... | collective-permute-start | bytes 442376 | tf_op jit(solution)/shard_map/ppermute | solution.py:222
  32.8 8.7 %collective-permute-start.7 = (bf16[128,576]{1,0:T(8,128)(2,1)S(1)}, bf16[128,576]{1,0:T(8,128)(2,1)}, u32[]{:S(2)}, u32[]{:S(2)}) collective-permute-start(bf16[128,576]{1,0:T(8,128)(2,1)S(1)} %add_convert_fusion.1), channel_id=1, source_target_pairs={{0,2},{1,3},{2,0},{3,1},{4,6},{5,7},{6,4},{7,5},{8,10},{9,11},{10,... | collective-permute-start | bytes 442376 | tf_op jit(solution)/shard_map/ppermute | solution.py:222
  33.3 8.3 %collective-permute-start.6 = (bf16[128,576]{1,0:T(8,128)(2,1)S(1)}, bf16[128,576]{1,0:T(8,128)(2,1)}, u32[]{:S(2)}, u32[]{:S(2)}) collective-permute-start(bf16[128,576]{1,0:T(8,128)(2,1)S(1)} %add_convert_fusion.1), channel_id=1, source_target_pairs={{0,1},{1,0},{2,3},{3,2},{4,5},{5,4},{6,7},{7,6},{8,9},{9,8},{10,11... | collective-permute-start | bytes 442376 | tf_op jit(solution)/shard_map/ppermute | solution.py:222
  33.9 12.8 %collective-permute-start.10 = (bf16[128,1792]{1,0:T(8,128)(2,1)S(1)}, bf16[128,1792]{1,0:T(8,128)(2,1)}, u32[]{:S(2)}, u32[]{:S(2)}) collective-permute-start(bf16[128,1792]{1,0:T(8,128)(2,1)S(1)} %copy-done), channel_id=1, source_target_pairs={{0,8},{4,12},{8,0},{12,4},{16,24},{20,28},{24,16},{28,20},{1,9},{5... | collective-permute-start | bytes 1376264 | tf_op jit(solution)/shard_map/ppermute | solution.py:166
  42.9 4.5 %collective-permute-start.9 = (bf16[128,256]{1,0:T(8,128)(2,1)S(1)}, bf16[128,256]{1,0:T(8,128)(2,1)S(1)}, u32[]{:S(2)}, u32[]{:S(2)}) collective-permute-start(bf16[128,256]{1,0:T(8,128)(2,1)S(1)} %pad_maximum_fusion.1), channel_id=1, source_target_pairs={{0,8},{4,12},{8,0},{12,4},{16,24},{20,28},{24,16},{28,20},{1,9},{5... | collective-permute-start | bytes 196616 | tf_op jit(solution)/shard_map/ppermute | solution.py:237
  49.1 1.9 %collective-permute-start.11 = (bf16[2,64,1792]{2,1,0:T(8,128)(2,1)S(1)}, bf16[2,64,1792]{2,1,0:T(8,128)(2,1)S(1)}, u32[]{:S(2)}, u32[]{:S(2)}) collective-permute-start(bf16[2,64,1792]{2,1,0:T(8,128)(2,1)S(1)} %get-tuple-element.26), channel_id=1, source_target_pairs={{0,4},{4,0},{8,12},{12,8},{16,20},{20,16},{24,28},{28,24},{1,5},{5... | collective-permute-start | bytes 1376264 | tf_op jit(solution)/shard_map/ppermute | solution.py:248
  51.1 9.6 %copy-start.1 = (f32[2,64,1792]{2,1,0:T(8,128)}, f32[2,64,1792]{2,1,0:T(8,128)S(1)}, u32[]{:S(2)}) copy-start(f32[2,64,1792]{2,1,0:T(8,128)S(1)} %convert_add_fusion) | copy-start | bytes 2752516
  51.2 13.5 %collective-permute-start.12 = (bf16[1,64,1792]{2,1,0:T(8,128)(2,1)S(1)}, bf16[1,64,1792]{2,1,0:T(8,128)(2,1)S(1)}, u32[]{:S(2)}, u32[]{:S(2)}) collective-permute-start(bf16[1,64,1792]{2,1,0:T(8,128)(2,1)S(1)} %slice.25), channel_id=1, source_target_pairs={{0,16},{4,20},{8,24},{12,28},{16,0},{20,4},{24,8},{28,12},{1,17},{... | collective-permute-start | bytes 688136 | tf_op jit(solution)/shard_map/ppermute | solution.py:251
